TPU v7x, 32 devices: a whole 2x2x4 slice. The times are simulated.
32 devices in a mesh: channel: 4 (over z), tm: 4 (over y, core), beam: 2 (over x).
Axes of the slice: x: 2, y: 2, z: 4, core: 2. Of those that a mesh axis runs over, the one named last changes fastest.
Arguments:
- voltages: bfloat16 [2, 2048, 64, 1024], P(None, ('beam', 'channel'), None, 'tm'), may hold values from -6 to 6
- positions: int32 [2048], replicated, may hold values from 0 to 1023
- delays: int32 [32, 1024], P(None, 'channel'), may hold values from 0 to 63
Outputs:
- intensity: float32 [1024, 64, 1024], P(('beam', 'tm'), 'channel')
- dedispersed: float32 [1024, 32, 64], P(('beam', 'tm'), 'channel')
Inputs may be any that keep to these rules, and one draw needn't show every extreme that they name: `positions`: place on a grid of 4 cylinders by 256 places along each.
All inputs are finite; a program needn't handle non-finite values.
Results may differ from a plain program's by a relative error of at most 0.0071.
Values may be sent and summed in bfloat16 or wider, within the bound.
No kernel may reach another device: no remote copies, remote signals or barrier semaphores. Data moves between devices by JAX's collectives and lax.ppermute only.
A program may use at most 192 MiB of HBM per device.

v0:
```python
import functools
import math

import jax
import jax.numpy as jnp
import numpy as np
from jax import lax
from jax.experimental import pallas as pl
from jax.experimental.pallas import tpu as pltpu
from jax.sharding import PartitionSpec as P


BEAMS = 1024
UPCH = 16
TAPS = 8
FINE = 1024
LANES = 128

TWO_PI = 2.0 * math.pi


def ring(value, axis, shift):
    count = lax.axis_size(axis)
    return lax.ppermute(value, axis, [(i, (i + shift) % count) for i in range(count)])


def stride(turn, parity, count):
    return 1 + (turn + 1 + 2 * parity) % (count - 1)


def partner(place, step, count):
    return place ^ step if count & (count - 1) == 0 else (step - place) % count


def exchange(value, turn):
    count, times = lax.axis_size("channel"), lax.axis_size("tm")
    pairs = [
        (i * times + t, partner(i, stride(turn, t % 2, count), count) * times + t)
        for i in range(count)
        for t in range(times)
    ]
    return lax.ppermute(value, ("channel", "tm"), pairs)


def steering(positions, beam_ids, places, feed_count):
    beam_east = beam_ids // places
    beam_north = beam_ids % places
    cylinder = positions // places
    along_row = positions % places
    coarse = (beam_east[:, None] * cylinder[None, :]) * (places // 4)
    steps = (coarse + beam_north[:, None] * along_row[None, :]) & (places - 1)
    quarter = places // 4
    side = (steps + quarter // 2) // quarter
    angle = (steps - side * quarter).astype(jnp.float32) * (TWO_PI / places)
    square = angle * angle
    sine = angle * (
        1.0 + square * (-1.0 / 6 + square * (1.0 / 120 + square * (-1.0 / 5040 + square / 362880)))
    )
    cosine = 1.0 + square * (
        -0.5 + square * (1.0 / 24 + square * (-1.0 / 720 + square * (1.0 / 40320 - square / 3628800)))
    )
    odd = (side & 1) == 1
    cos_part = jnp.where(odd, sine, cosine)
    sin_part = jnp.where(odd, cosine, sine)
    norm_scale = 1.0 / math.sqrt(feed_count)
    cos_sign = jnp.where(((side + 1) & 2) == 0, norm_scale, -norm_scale)
    sin_sign = jnp.where((side & 2) == 0, norm_scale, -norm_scale)
    w_real = (cos_part * cos_sign).astype(jnp.bfloat16)
    w_imag = (-sin_part * sin_sign).astype(jnp.bfloat16)
    return w_real, w_imag


def filter_matrices():
    length = TAPS * UPCH
    index = np.arange(length, dtype=np.float64)
    taper = np.sinc((index - (length - 1) / 2.0) / UPCH) * (
        0.5 - 0.5 * np.cos(TWO_PI * (index + 0.5) / length)
    )
    taper = taper / np.sqrt(np.sum(taper * taper))
    frames = LANES // UPCH
    mats = []
    for first in (-LANES, 0):
        sample = np.arange(first, first + LANES)
        inner = sample % UPCH
        tap = (sample - inner)[:, None] // UPCH - np.arange(frames)[None, :] + TAPS - 1
        inside = (tap >= 0) & (tap < TAPS)
        gain = np.where(inside, taper[np.clip(tap, 0, TAPS - 1) * UPCH + inner[:, None]], 0.0)
        phase = TWO_PI * (inner[:, None] * np.arange(UPCH)[None, :] % UPCH) / UPCH
        real = (gain[:, :, None] * np.cos(phase)[:, None, :]).reshape(LANES, LANES)
        imag = (gain[:, :, None] * -np.sin(phase)[:, None, :]).reshape(LANES, LANES)
        full = np.concatenate(
            [np.concatenate([real, imag], axis=1), np.concatenate([-imag, real], axis=1)], axis=0
        )
        high = full.astype(jnp.bfloat16)
        low = (full - high.astype(np.float64)).astype(jnp.bfloat16)
        mats.append(np.concatenate([high, low], axis=1))
    return np.stack(mats)


def frame_distance(frames):
    row = np.arange(frames)[:, None]
    col = np.arange(frames * UPCH)[None, :] // UPCH
    return ((row - col) % frames).astype(np.int32)


def spread_kernel(index_ref, v_ref, order_ref, *out_refs):
    step, width, samples = v_ref.shape
    rows = order_ref.shape[0]
    take = rows // width
    for f in range(step // take):
        part = v_ref[f * take : (f + 1) * take].reshape(rows, samples)
        moved = jnp.dot(order_ref[...], part, preferred_element_type=jnp.float32).astype(v_ref.dtype)
        c = 0
        for out_ref in out_refs:
            for i in range(out_ref.shape[0]):
                out_ref[i, f * take : (f + 1) * take, :] = moved[c * take : (c + 1) * take]
                c += 1


def spread(voltages, index, sizes):
    parts, feeds, _, samples = voltages.shape
    width = sum(sizes)
    take = math.gcd(feeds, 256 // width)
    step = math.gcd(feeds, 8 * take)
    cuts = feeds // step
    rows = take * width
    order = np.zeros((rows, rows), np.float32)
    for c in range(width):
        for f in range(take):
            order[c * take + f, f * width + c] = 1.0
    return pl.pallas_call(
        spread_kernel,
        grid_spec=pltpu.PrefetchScalarGridSpec(
            num_scalar_prefetch=1,
            grid=(parts, cuts),
            in_specs=[
                pl.BlockSpec((None, step, width, samples), lambda r, f, index: (r, f, index[0], 0)),
                pl.BlockSpec((rows, rows), lambda r, f, index: (0, 0)),
            ],
            out_specs=[
                pl.BlockSpec((size, step, samples), lambda r, f, index: (0, r * cuts + f, 0))
                for size in sizes
            ],
        ),
        out_shape=[
            jax.ShapeDtypeStruct((size, parts * feeds, samples), voltages.dtype) for size in sizes
        ],
        name="spread",
    )(index, voltages, jnp.asarray(order, voltages.dtype))


def partial_kernel(*refs):
    w_ref, *v_refs, _, out_ref = refs
    total = None
    for s, v_ref in enumerate(v_refs):
        part = jnp.dot(w_ref[s], v_ref[...], preferred_element_type=jnp.float32)
        total = part if total is None else total + part
    out_ref[...] = total.astype(out_ref.dtype)


def after():
    return pl.BlockSpec(memory_space=pl.ANY)


def beam_partial(weights, pieces, token):
    sources, rows, cols = weights.shape
    chans, _, samples = pieces[0].shape
    return pl.pallas_call(
        partial_kernel,
        grid=(chans,),
        in_specs=[pl.BlockSpec((sources, rows, cols), lambda c: (0, 0, 0))]
        + [pl.BlockSpec((None, cols, samples), lambda c: (c, 0, 0)) for _ in pieces]
        + [after()],
        out_specs=pl.BlockSpec((None, rows, samples), lambda c: (c, 0, 0)),
        out_shape=jax.ShapeDtypeStruct((chans, rows, samples), jnp.bfloat16),
        name="beam_partial",
        cost_estimate=pl.CostEstimate(
            flops=2 * chans * rows * sources * cols * samples,
            bytes_accessed=2 * (sources * rows * cols + chans * samples * (sources * cols + rows)),
            transcendentals=0,
        ),
    )(weights, *pieces, token)


def own_kernel(n_pieces, n_received, *refs):
    w_ref = refs[0]
    v_refs = refs[1 : 1 + n_pieces]
    r_refs = refs[1 + n_pieces : 1 + n_pieces + n_received]
    out_refs = refs[2 + n_pieces + n_received :]
    total = None
    for s, v_ref in enumerate(v_refs):
        part = jnp.dot(w_ref[s], v_ref[...], preferred_element_type=jnp.float32)
        total = part if total is None else total + part
    for r_ref in r_refs:
        total = total + r_ref[...].astype(jnp.float32)
    beams = total.astype(jnp.bfloat16)
    held = beams.shape[0] // 2
    each = held // len(out_refs)
    for j, out_ref in enumerate(out_refs):
        for a in range(out_ref.shape[0]):
            lanes = slice(a * LANES, (a + 1) * LANES)
            out_ref[a, :, :LANES] = beams[j * each : (j + 1) * each, lanes]
            out_ref[a, :, LANES:] = beams[held + j * each : held + (j + 1) * each, lanes]


def own_beams(weights, pieces, received, blocks, token):
    sources, rows, cols = weights.shape
    chans, _, samples = pieces[0].shape
    each = rows // 2 // blocks
    tiles = samples // LANES
    return pl.pallas_call(
        functools.partial(own_kernel, len(pieces), len(received)),
        grid=(chans,),
        in_specs=[pl.BlockSpec((sources, rows, cols), lambda c: (0, 0, 0))]
        + [pl.BlockSpec((None, cols, samples), lambda c: (c, 0, 0)) for _ in pieces]
        + [pl.BlockSpec((None, rows, samples), lambda c: (c, 0, 0)) for _ in received]
        + [after()],
        out_specs=[
            pl.BlockSpec((None, tiles, each, 2 * LANES), lambda c: (c, 0, 0, 0))
            for _ in range(blocks)
        ],
        out_shape=[
            jax.ShapeDtypeStruct((chans, tiles, each, 2 * LANES), jnp.bfloat16)
            for _ in range(blocks)
        ],
        name="own_beams",
        cost_estimate=pl.CostEstimate(
            flops=2 * chans * rows * sources * cols * samples,
            bytes_accessed=2 * (sources * rows * cols + chans * samples * (sources * cols + 3 * rows)),
            transcendentals=0,
        ),
    )(weights, *pieces, *received, token)


def spectrum_kernel(n_blocks, trial_block, last, *refs):
    me_ref = refs[0]
    in_refs = refs[1 : 1 + n_blocks]
    h_ref, dist_ref, delay_ref, acc_in = refs[1 + n_blocks : 5 + n_blocks]
    n_out = 1 + n_out_of(last)
    power_ref, *sum_refs = refs[6 + n_blocks : 6 + n_blocks + n_out]
    x_ref, c_ref, hot_ref, acc_ref = refs[6 + n_blocks + n_out :]
    step = pl.program_id(0)
    tiles, each, width = in_refs[0].shape
    all_tiles = n_blocks * tiles
    frames = all_tiles * (LANES // UPCH)
    trials = delay_ref.shape[0]

    x_ref[:each, :] = jnp.zeros((each, width), x_ref.dtype)
    for j, in_ref in enumerate(in_refs):
        block = lax.rem(me_ref[0] + (n_blocks - j), n_blocks)
        start = pl.multiple_of((1 + block * tiles) * each, each)
        x_ref[pl.ds(start, tiles * each), :] = in_ref[...].reshape(tiles * each, width)
    spectra = jnp.dot(x_ref[each:, :], h_ref[1], preferred_element_type=jnp.float32) + jnp.dot(
        x_ref[: all_tiles * each, :], h_ref[0], preferred_element_type=jnp.float32
    )
    real = spectra[:, :LANES] + spectra[:, 2 * LANES : 3 * LANES]
    imag = spectra[:, LANES : 2 * LANES] + spectra[:, 3 * LANES :]
    power = real * real + imag * imag
    mean = power[:each]
    for i in range(1, all_tiles):
        mean = mean + power[i * each : (i + 1) * each]
    shift = LANES // 2
    while shift >= UPCH:
        mean = mean + pltpu.roll(mean, shift, 1)
        shift //= 2
    mean = mean * (1.0 / frames)
    for i in range(all_tiles):
        lanes = slice(i * LANES, (i + 1) * LANES)
        tile = power[i * each : (i + 1) * each]
        power_ref[:, lanes] = tile
        centred = tile - mean
        high = centred.astype(jnp.bfloat16)
        c_ref[:each, lanes] = high
        c_ref[each:, lanes] = (centred - high.astype(jnp.float32)).astype(jnp.bfloat16)

    @pl.when(step == 0)
    def _():
        acc_ref[...] = jnp.zeros(acc_ref.shape, jnp.float32)

    def trial_group(g, carry):
        for i in range(all_tiles):
            lanes = slice(i * LANES, (i + 1) * LANES)
            dist = dist_ref[:, lanes]
            for d in range(trial_block):
                wanted = delay_ref[pl.ds(g * trial_block + d, 1), :]
                hot_ref[d * frames : (d + 1) * frames, lanes] = jnp.where(
                    dist == wanted, 1.0, 0.0
                ).astype(jnp.bfloat16)
        rows = pl.ds(pl.multiple_of(g * (trial_block * frames), trial_block * frames), trial_block * frames)
        acc_ref[rows, :] += lax.dot_general(
            hot_ref[...], c_ref[...], (((1,), (1,)), ((), ())), preferred_element_type=jnp.float32
        )
        return carry

    lax.fori_loop(0, trials // trial_block, trial_group, 0)

    @pl.when(step == pl.num_programs(0) - 1)
    def _():
        rows = acc_ref.shape[0] // len(sum_refs)
        for s, sum_ref in enumerate(sum_refs):
            part = slice(s * rows, (s + 1) * rows)
            total = acc_ref[part, :each] + acc_ref[part, each:] + acc_in[part, :]
            sum_ref[...] = total.astype(sum_ref.dtype)


def n_out_of(last):
    return last if last else 1


def spectrum(me, blocks, matrices, distance, delay_rows, start, sums, last, token):
    chans, tiles, each, width = blocks[0].shape
    samples = len(blocks) * tiles * LANES
    frames = samples // UPCH
    trials = delay_rows.shape[1]
    trial_block = math.gcd(trials, 8)
    n_sums = n_out_of(last)
    rows = trials * frames // n_sums
    whole = lambda shape: pl.BlockSpec(shape, lambda c, me: (0,) * len(shape))
    out = pl.pallas_call(
        functools.partial(spectrum_kernel, len(blocks), trial_block, last),
        grid_spec=pltpu.PrefetchScalarGridSpec(
            num_scalar_prefetch=1,
            grid=(chans,),
            in_specs=[
                pl.BlockSpec((None, tiles, each, width), lambda c, me: (c, 0, 0, 0)) for _ in blocks
            ]
            + [
                whole(matrices.shape),
                whole(distance.shape),
                pl.BlockSpec((None, trials, LANES), lambda c, me: (start + c, 0, 0)),
                whole(sums.shape),
                after(),
            ],
            out_specs=[pl.BlockSpec((None, each, samples), lambda c, me: (c, 0, 0))]
            + [whole((rows, each)) for _ in range(n_sums)],
            scratch_shapes=[
                pltpu.VMEM(((1 + len(blocks) * tiles) * each, width), jnp.bfloat16),
                pltpu.VMEM((2 * each, samples), jnp.bfloat16),
                pltpu.VMEM((trial_block * frames, samples), jnp.bfloat16),
                pltpu.VMEM((trials * frames, 2 * each), jnp.float32),
            ],
        ),
        out_shape=[jax.ShapeDtypeStruct((chans, each, samples), jnp.float32)]
        + [
            jax.ShapeDtypeStruct((rows, each), jnp.bfloat16 if s else jnp.float32)
            for s in range(n_sums)
        ],
        name="spectrum",
        cost_estimate=pl.CostEstimate(
            flops=4 * chans * each * samples * (trials * frames + 8 * LANES),
            bytes_accessed=8 * chans * each * samples,
            transcendentals=0,
        ),
    )(me, *blocks, matrices, distance, delay_rows, sums, token)
    return out[0], out[1:]


def place_kernel(n_chunks, *refs):
    out_ref = refs[-1]
    c = 0
    for in_ref in refs[:n_chunks]:
        for i in range(in_ref.shape[0]):
            out_ref[:, c, :] = in_ref[i]
            c += 1


def place(chunks, group, channels, held):
    _, beams, samples = chunks[0].shape
    width = sum(chunk.shape[0] for chunk in chunks)
    step = math.gcd(beams, 16)
    shape = (beams, channels, samples)
    return pl.pallas_call(
        functools.partial(place_kernel, len(chunks)),
        grid=(beams // step,),
        in_specs=[pl.BlockSpec((chunk.shape[0], step, samples), lambda b: (0, b, 0)) for chunk in chunks]
        + [pl.BlockSpec(memory_space=pl.ANY) for _ in held],
        out_specs=pl.BlockSpec((step, width, samples), lambda b: (b, group, 0)),
        out_shape=jax.ShapeDtypeStruct(shape, jnp.float32),
        input_output_aliases={len(chunks): 0} if held else {},
        name="place",
    )(*chunks, *held)


def chunk_sizes(count):
    eighth = count // 8
    if not eighth:
        return [1] * count
    rest = count - 7 * eighth
    small = max(1, rest // 2)
    return [eighth] * 7 + [rest - small, small]


def grouped_sizes(sizes, block):
    groups, filled = [[]], 0
    for size in sizes:
        groups[-1].append(size)
        filled += size
        if filled > block:
            return None
        if filled == block:
            groups.append([])
            filled = 0
    return groups[:-1] if filled == 0 else None


def per_device(voltages, positions, delays):
    places = BEAMS // 4
    n_chan = lax.axis_size("channel")
    n_time = lax.axis_size("tm")
    n_beam = lax.axis_size("beam")
    my_chan = lax.axis_index("channel")
    my_time = lax.axis_index("tm")
    my_beam = lax.axis_index("beam")
    _, feeds, channels, samples = voltages.shape
    own_channels = channels // n_chan
    half_beams = BEAMS // n_beam
    own_count = half_beams // n_time
    frames = n_time * samples // UPCH
    trials = delays.shape[0]
    sizes = chunk_sizes(own_channels)
    starts = [sum(sizes[:i]) for i in range(len(sizes))]

    groups = grouped_sizes(sizes, 8)
    targets = [my_chan] + [
        partner(my_chan, stride(turn, my_time % 2, n_chan), n_chan) for turn in range(n_chan - 1)
    ]
    by_target = [[] for _ in targets]
    if groups is None:
        by_channel = jnp.transpose(voltages, (2, 0, 1, 3)).reshape(channels, 2 * feeds, samples)
        for start, size in zip(starts, sizes):
            for s, target in enumerate(targets):
                piece = lax.dynamic_slice_in_dim(by_channel, target * own_channels + start, size, 0)
                by_target[s].append(piece)
    else:
        for g, group in enumerate(groups):
            for s in [*range(1, n_chan), 0]:
                index = targets[s] * (own_channels // 8) + g
                by_target[s] += spread(voltages, index.astype(jnp.int32).reshape(1), group)
    pieces = []
    for i in range(len(sizes)):
        chunk = [by_target[0][i]]
        for s in range(1, n_chan):
            chunk.append(exchange(by_target[s][i], s - 1))
        pieces.append(chunk)
    leaving = [by_target[s][0] for s in range(1, n_chan)]
    positions, _ = lax.optimization_barrier((positions, leaving))

    grouped = positions.reshape(n_beam, n_chan, feeds)[my_beam]
    near = grouped[jnp.stack(targets)].reshape(-1)
    block_ids = (my_time + jnp.arange(n_time)) % n_time
    local_ids = (block_ids[:, None] * own_count + jnp.arange(own_count)[None, :]).reshape(-1)
    weights = []
    for s in range(n_beam):
        beam_ids = (my_beam + s) % n_beam * half_beams + local_ids
        w_real, w_imag = steering(near, beam_ids, places, positions.shape[0])
        shape = (half_beams, n_chan, feeds)
        w_real = jnp.transpose(w_real.reshape(shape), (1, 0, 2))
        w_imag = jnp.transpose(w_imag.reshape(shape), (1, 0, 2))
        weights.append(
            jnp.concatenate(
                [
                    jnp.concatenate([w_real, -w_imag], axis=2),
                    jnp.concatenate([w_imag, w_real], axis=2),
                ],
                axis=1,
            )
        )

    matrices = jnp.asarray(filter_matrices())
    distance = jnp.asarray(frame_distance(frames))
    trial_order = (my_chan + jnp.arange(n_chan)) % n_chan
    delay_rows = delays.reshape(n_chan, trials // n_chan, own_channels, UPCH)[trial_order]
    delay_rows = jnp.transpose(delay_rows, (2, 0, 1, 3)).reshape(own_channels, trials, UPCH)
    delay_rows = jnp.tile(delay_rows, (1, 1, LANES // UPCH))
    me = my_time.astype(jnp.int32).reshape(1)

    powers = []
    sums = jnp.zeros((trials * frames, own_count), jnp.float32)
    received, blocks = {}, {}
    last = len(pieces) - 1
    token = by_target[-1][-1]
    for step in range(len(pieces) + 2):
        index = step
        if index <= last:
            received[index] = []
            for s in range(1, n_beam):
                token = beam_partial(weights[s], pieces[index], token)
                received[index].append(ring(token, "beam", s))
        index = step - 1
        if 0 <= index <= last:
            turned = own_beams(weights[0], pieces[index], received[index], n_time, token)
            token = turned[0]
            blocks[index] = [turned[0]]
            for j in range(1, n_time):
                blocks[index].append(ring(turned[j], "tm", j))
        index = step - 2
        if 0 <= index:
            power, out_sums = spectrum(
                me,
                blocks[index],
                matrices,
                distance,
                delay_rows,
                starts[index],
                sums,
                n_chan if index == last else 0,
                token,
            )
            powers.append(power)
            sums = out_sums[0]
            token = power
    total = sums
    for s in range(1, n_chan):
        total = total + ring(out_sums[s], "channel", s).astype(jnp.float32)
    total = total * (1.0 / math.sqrt(FINE))
    dedispersed = jnp.transpose(
        total.reshape(trials // n_chan, frames, own_count), (2, 0, 1)
    )
    if groups is None:
        intensity = jnp.transpose(jnp.concatenate(powers, axis=0), (1, 0, 2))
    else:
        held = []
        for g, group in enumerate(groups):
            held = [place(powers[: len(group)], g, own_channels, held)]
            powers = powers[len(group) :]
        intensity = held[0]
    return (intensity, dedispersed)


def solution(mesh):
    return jax.shard_map(
        per_device,
        mesh=mesh,
        in_specs=(P(None, ("beam", "channel"), None, "tm"), P(), P(None, "channel")),
        out_specs=(P(("beam", "tm"), "channel", None), P(("beam", "tm"), "channel", None)),
        check_vma=False,
    )
```

profile of v0, /device:TPU:0, one launch (start us, length us, event | category | flops | bytes accessed | tf_op | source)
XLA Modules:
  0.0 498.3 jit_solution(6604491084346932560)
XLA Ops:
  20.5 10.1 %multiply_convert_fusion = (bf16[4,512,256]{2,1,0:T(8,128)(2,1)}, bf16[4,512,256]{2,1,0:T(8,128)(2,1)}, bf16[4,512,256]{2,1,0:T(8,128)(2,1)S(1)}, bf16[4,512,256]{2,1,0:T(8,128)(2,1)}) fusion(s32[512]{0:T(512)S(1)} %get-tuple-element.203, s32[512]{0:T(512)S(1)} %get-tuple-element.200, s32[4,256]{1,0:T(4,128)S(1)} %get-tuple-element.199, ...), kind=kLoop, calls=%fused_computation.14 | loop fusion | flops 63963136 | bytes 4210688 | tf_op jit(solution)/shard_map/convert_element_type | solution.py:69
  30.6 8.4 %fusion.27 = (bf16[4,512,256]{2,1,0:T(8,128)(2,1)S(1)}, bf16[4,512,256]{2,1,0:T(8,128)(2,1)S(1)}) fusion(s32[4,256]{1,0:T(4,128)S(1)} %get-tuple-element.199, s32[512]{0:T(512)S(1)} %get-tuple-element.203, s32[4,256]{1,0:T(4,128)S(1)} %get-tuple-element.198, s32[512]{0:T(512)S(1)} %get-tuple-element.200, s32[512]{0:T(512)S(1)} %get-tuple-element.202, ...), kind=kLoop, calls=%fused_computation.97 | loop fusion | flops 59768832 | bytes 2113536 | tf_op jit(solution)/shard_map/neg | solution.py:462
  49.8 27.0 %collective-permute-done.6.refs_2_ = bf16[2,512,256]{2,1,0:T(8,128)(2,1)} collective-permute-done((bf16[2,512,256]{2,1,0:T(8,128)(2,1)}, bf16[2,512,256]{2,1,0:T(8,128)(2,1)}, u32[]{:S(2)}, u32[]{:S(2)}) %collective-permute-start.6) | collective-permute-done | bytes 524320 | tf_op jit(solution)/shard_map/ppermute | solution.py:42
  84.0 14.8 %collective-permute-done.3.refs_2_ = bf16[2,512,256]{2,1,0:T(8,128)(2,1)S(1)} collective-permute-done((bf16[2,512,256]{2,1,0:T(8,128)(2,1)}, bf16[2,512,256]{2,1,0:T(8,128)(2,1)S(1)}, u32[]{:S(2)}, u32[]{:S(2)}) %collective-permute-start.3) | collective-permute-done | bytes 524320 | tf_op jit(solution)/shard_map/ppermute | solution.py:42
  99.6 6.0 %beam_partial.10.refs_6_ = bf16[2,1024,256]{2,1,0:T(8,128)(2,1)} custom-call(bf16[4,1024,512]{2,1,0:T(8,128)(2,1)} %maximum_maximum_fusion.1.refs_0_, bf16[2,512,256]{2,1,0:T(8,128)(2,1)} %get-tuple-element.104.refs_1_, bf16[2,512,256]{2,1,0:T(8,128)(2,1)} %copy-done.10, bf16[2,512,256]{2,1,0:T(8,128)(2,1)} %collective-permute-done.4.refs_3_, ...), custom_call_target="tpu_custom_call" | custom-call | flops 2147483648 | bytes 7340032 | tf_op jit(solution)/shard_map/beam_partial/pallas_call | solution.py:168
  117.2 6.2 %own_beams.9 = (bf16[2,2,128,256]{3,2,1,0:T(8,128)(2,1)}, bf16[2,2,128,256]{3,2,1,0:T(8,128)(2,1)}, bf16[2,2,128,256]{3,2,1,0:T(8,128)(2,1)}, bf16[2,2,128,256]{3,2,1,0:T(8,128)(2,1)}) custom-call(bf16[4,1024,512]{2,1,0:T(8,128)(2,1)} %maximum_maximum_fusion.refs_0_, bf16[2,512,256]{2,1,0:T(8,128)(2,1)} %get-tuple-element.108.refs_1_, ...), custom_call_target="tpu_custom_call" | custom-call | flops 2147483648 | bytes 9437184 | tf_op jit(solution)/shard_map/own_beams/pallas_call | solution.py:211
  124.3 18.1 %collective-permute-start.17 = (bf16[2,2,128,256]{3,2,1,0:T(8,128)(2,1)}, bf16[2,2,128,256]{3,2,1,0:T(8,128)(2,1)S(1)}, u32[]{:S(2)}, u32[]{:S(2)}) collective-permute-start(bf16[2,2,128,256]{3,2,1,0:T(8,128)(2,1)} %get-tuple-element.119), channel_id=1, source_target_pairs={{0,2},{2,4},{4,6},{6,0},{1,3},{3,5},{5,7},{7,1},{8,10},{10,12},{12... | collective-permute-start | bytes 786440 | tf_op jit(solution)/shard_map/ppermute | solution.py:24
  142.4 30.6 %collective-permute-done.10.refs_2_ = bf16[2,512,256]{2,1,0:T(8,128)(2,1)} collective-permute-done((bf16[2,512,256]{2,1,0:T(8,128)(2,1)}, bf16[2,512,256]{2,1,0:T(8,128)(2,1)}, u32[]{:S(2)}, u32[]{:S(2)}) %collective-permute-start.10) | collective-permute-done | bytes 524320 | tf_op jit(solution)/shard_map/ppermute | solution.py:42
  173.0 6.0 %beam_partial.11.refs_6_ = bf16[2,1024,256]{2,1,0:T(8,128)(2,1)} custom-call(bf16[4,1024,512]{2,1,0:T(8,128)(2,1)} %maximum_maximum_fusion.1.refs_0_, bf16[2,512,256]{2,1,0:T(8,128)(2,1)} %get-tuple-element.110.refs_1_, bf16[2,512,256]{2,1,0:T(8,128)(2,1)} %collective-permute-done.10.refs_2_, bf16[2,512,256]{2,1,0:T(8,128)(2,1)} %collective-permute-done.11.refs_3_, ...), custom_call_target="tpu_custom_call" | custom-call | flops 2147483648 | bytes 7340032 | tf_op jit(solution)/shard_map/beam_partial/pallas_call | solution.py:168
  188.4 6.2 %own_beams.10 = (bf16[2,2,128,256]{3,2,1,0:T(8,128)(2,1)}, bf16[2,2,128,256]{3,2,1,0:T(8,128)(2,1)}, bf16[2,2,128,256]{3,2,1,0:T(8,128)(2,1)}, bf16[2,2,128,256]{3,2,1,0:T(8,128)(2,1)}) custom-call(bf16[4,1024,512]{2,1,0:T(8,128)(2,1)} %maximum_maximum_fusion.refs_0_, bf16[2,512,256]{2,1,0:T(8,128)(2,1)} %get-tuple-element.104.refs_1_, ...), custom_call_target="tpu_custom_call" | custom-call | flops 2147483648 | bytes 9437184 | tf_op jit(solution)/shard_map/own_beams/pallas_call | solution.py:211
  196.4 9.3 %spectrum.9 = (f32[2,128,1024]{2,1,0:T(8,128)}, f32[2048,128]{1,0:T(8,128)}) custom-call(s32[1]{0:T(128)} %bitcast.refs_0_, bf16[2,2,128,256]{3,2,1,0:T(8,128)(2,1)} %get-tuple-element.114.refs_5_.refs_1_, bf16[2,2,128,256]{3,2,1,0:T(8,128)(2,1)} %copy-done.41, bf16[2,2,128,256]{3,2,1,0:T(8,128)(2,1)} %collective-permute-done.18.refs_3_, ...), custom_call_target="tpu_custom_call" | custom-call | flops 3221225472 | bytes 2097152 | tf_op jit(solution)/shard_map/spectrum/pallas_call | solution.py:319
  207.9 6.0 %beam_partial.12.refs_6_ = bf16[2,1024,256]{2,1,0:T(8,128)(2,1)} custom-call(bf16[4,1024,512]{2,1,0:T(8,128)(2,1)} %maximum_maximum_fusion.1.refs_0_, bf16[2,512,256]{2,1,0:T(8,128)(2,1)} %get-tuple-element.123.refs_1_, bf16[2,512,256]{2,1,0:T(8,128)(2,1)} %copy-done.3, bf16[2,512,256]{2,1,0:T(8,128)(2,1)} %copy-done.1, bf16[2,512,256]{2,1,0:T(8,128)(2,1)} %copy-done.2, ...), custom_call_target="tpu_custom_call" | custom-call | flops 2147483648 | bytes 7340032 | tf_op jit(solution)/shard_map/beam_partial/pallas_call | solution.py:168
  228.3 6.3 %own_beams.11 = (bf16[2,2,128,256]{3,2,1,0:T(8,128)(2,1)}, bf16[2,2,128,256]{3,2,1,0:T(8,128)(2,1)}, bf16[2,2,128,256]{3,2,1,0:T(8,128)(2,1)}, bf16[2,2,128,256]{3,2,1,0:T(8,128)(2,1)}) custom-call(bf16[4,1024,512]{2,1,0:T(8,128)(2,1)} %maximum_maximum_fusion.refs_0_, bf16[2,512,256]{2,1,0:T(8,128)(2,1)} %get-tuple-element.110.refs_1_, ...), custom_call_target="tpu_custom_call" | custom-call | flops 2147483648 | bytes 9437184 | tf_op jit(solution)/shard_map/own_beams/pallas_call | solution.py:211
  237.4 9.3 %spectrum.10 = (f32[2,128,1024]{2,1,0:T(8,128)}, f32[2048,128]{1,0:T(8,128)}) custom-call(s32[1]{0:T(128)} %bitcast.refs_0_, bf16[2,2,128,256]{3,2,1,0:T(8,128)(2,1)} %get-tuple-element.115.refs_9_.refs_1_, bf16[2,2,128,256]{3,2,1,0:T(8,128)(2,1)} %copy-done.36, bf16[2,2,128,256]{3,2,1,0:T(8,128)(2,1)} %copy-done.37, ...), custom_call_target="tpu_custom_call" | custom-call | flops 3221225472 | bytes 2097152 | tf_op jit(solution)/shard_map/spectrum/pallas_call | solution.py:319
  246.7 6.6 %collective-permute-done.2.refs_4_ = bf16[2,512,256]{2,1,0:T(8,128)(2,1)S(1)} collective-permute-done((bf16[2,512,256]{2,1,0:T(8,128)(2,1)}, bf16[2,512,256]{2,1,0:T(8,128)(2,1)S(1)}, u32[]{:S(2)}, u32[]{:S(2)}) %collective-permute-start.2) | collective-permute-done | bytes 524320 | tf_op jit(solution)/shard_map/ppermute | solution.py:42
  253.3 27.7 %collective-permute-done.refs_2_ = bf16[2,512,256]{2,1,0:T(8,128)(2,1)S(1)} collective-permute-done((bf16[2,512,256]{2,1,0:T(8,128)(2,1)}, bf16[2,512,256]{2,1,0:T(8,128)(2,1)S(1)}, u32[]{:S(2)}, u32[]{:S(2)}) %collective-permute-start) | collective-permute-done | bytes 524320 | tf_op jit(solution)/shard_map/ppermute | solution.py:42
  281.7 6.0 %beam_partial.13.refs_6_ = bf16[2,1024,256]{2,1,0:T(8,128)(2,1)} custom-call(bf16[4,1024,512]{2,1,0:T(8,128)(2,1)} %maximum_maximum_fusion.1.refs_0_, bf16[2,512,256]{2,1,0:T(8,128)(2,1)} %get-tuple-element.100.refs_1_, bf16[2,512,256]{2,1,0:T(8,128)(2,1)} %copy-done.7, bf16[2,512,256]{2,1,0:T(8,128)(2,1)} %copy-done.5, bf16[2,512,256]{2,1,0:T(8,128)(2,1)} %copy-done.6, ...), custom_call_target="tpu_custom_call" | custom-call | flops 2147483648 | bytes 7340032 | tf_op jit(solution)/shard_map/beam_partial/pallas_call | solution.py:168
  297.5 6.3 %own_beams.12 = (bf16[2,2,128,256]{3,2,1,0:T(8,128)(2,1)}, bf16[2,2,128,256]{3,2,1,0:T(8,128)(2,1)}, bf16[2,2,128,256]{3,2,1,0:T(8,128)(2,1)}, bf16[2,2,128,256]{3,2,1,0:T(8,128)(2,1)}) custom-call(bf16[4,1024,512]{2,1,0:T(8,128)(2,1)} %maximum_maximum_fusion.refs_0_, bf16[2,512,256]{2,1,0:T(8,128)(2,1)} %get-tuple-element.123.refs_1_, ...), custom_call_target="tpu_custom_call" | custom-call | flops 2147483648 | bytes 9437184 | tf_op jit(solution)/shard_map/own_beams/pallas_call | solution.py:211
  304.6 9.3 %spectrum.11 = (f32[2,128,1024]{2,1,0:T(8,128)}, f32[2048,128]{1,0:T(8,128)}) custom-call(s32[1]{0:T(128)} %bitcast.refs_0_, bf16[2,2,128,256]{3,2,1,0:T(8,128)(2,1)} %get-tuple-element.128.refs_9_.refs_1_, bf16[2,2,128,256]{3,2,1,0:T(8,128)(2,1)} %copy-done.49, bf16[2,2,128,256]{3,2,1,0:T(8,128)(2,1)} %copy-done.50, ...), custom_call_target="tpu_custom_call" | custom-call | flops 3221225472 | bytes 2097152 | tf_op jit(solution)/shard_map/spectrum/pallas_call | solution.py:319
  319.7 6.0 %beam_partial.14.refs_6_ = bf16[2,1024,256]{2,1,0:T(8,128)(2,1)} custom-call(bf16[4,1024,512]{2,1,0:T(8,128)(2,1)} %maximum_maximum_fusion.1.refs_0_, bf16[2,512,256]{2,1,0:T(8,128)(2,1)} %get-tuple-element.130.refs_1_, bf16[2,512,256]{2,1,0:T(8,128)(2,1)} %copy-done.9, bf16[2,512,256]{2,1,0:T(8,128)(2,1)} %copy-done.4, bf16[2,512,256]{2,1,0:T(8,128)(2,1)} %copy-done.8, ...), custom_call_target="tpu_custom_call" | custom-call | flops 2147483648 | bytes 7340032 | tf_op jit(solution)/shard_map/beam_partial/pallas_call | solution.py:168
  329.5 6.2 %own_beams.13 = (bf16[2,2,128,256]{3,2,1,0:T(8,128)(2,1)}, bf16[2,2,128,256]{3,2,1,0:T(8,128)(2,1)}, bf16[2,2,128,256]{3,2,1,0:T(8,128)(2,1)}, bf16[2,2,128,256]{3,2,1,0:T(8,128)(2,1)}) custom-call(bf16[4,1024,512]{2,1,0:T(8,128)(2,1)} %maximum_maximum_fusion.refs_0_, bf16[2,512,256]{2,1,0:T(8,128)(2,1)} %get-tuple-element.100.refs_1_, ...), custom_call_target="tpu_custom_call" | custom-call | flops 2147483648 | bytes 9437184 | tf_op jit(solution)/shard_map/own_beams/pallas_call | solution.py:211
  335.7 9.3 %spectrum.12 = (f32[2,128,1024]{2,1,0:T(8,128)}, f32[2048,128]{1,0:T(8,128)}) custom-call(s32[1]{0:T(128)} %bitcast.refs_0_, bf16[2,2,128,256]{3,2,1,0:T(8,128)(2,1)} %get-tuple-element.138.refs_9_.refs_1_, bf16[2,2,128,256]{3,2,1,0:T(8,128)(2,1)} %copy-done.46, bf16[2,2,128,256]{3,2,1,0:T(8,128)(2,1)} %copy-done.47, ...), custom_call_target="tpu_custom_call" | custom-call | flops 3221225472 | bytes 2097152 | tf_op jit(solution)/shard_map/spectrum/pallas_call | solution.py:319
  347.2 15.8 %collective-permute-done.39.refs_2_ = bf16[2,512,256]{2,1,0:T(8,128)(2,1)S(1)} collective-permute-done((bf16[2,512,256]{2,1,0:T(8,128)(2,1)}, bf16[2,512,256]{2,1,0:T(8,128)(2,1)S(1)}, u32[]{:S(2)}, u32[]{:S(2)}) %collective-permute-start.39) | collective-permute-done | bytes 524320 | tf_op jit(solution)/shard_map/ppermute | solution.py:42
  363.8 6.0 %beam_partial.15.refs_6_ = bf16[2,1024,256]{2,1,0:T(8,128)(2,1)} custom-call(bf16[4,1024,512]{2,1,0:T(8,128)(2,1)} %maximum_maximum_fusion.1.refs_0_, bf16[2,512,256]{2,1,0:T(8,128)(2,1)} %get-tuple-element.149.refs_1_, bf16[2,512,256]{2,1,0:T(8,128)(2,1)} %copy-done.21, bf16[2,512,256]{2,1,0:T(8,128)(2,1)} %copy-done.19, bf16[2,512,256]{2,1,0:T(8,128)(2,1)} %copy-done.20, ...), custom_call_target="tpu_custom_call" | custom-call | flops 2147483648 | bytes 7340032 | tf_op jit(solution)/shard_map/beam_partial/pallas_call | solution.py:168
  374.5 6.2 %own_beams.14 = (bf16[2,2,128,256]{3,2,1,0:T(8,128)(2,1)}, bf16[2,2,128,256]{3,2,1,0:T(8,128)(2,1)}, bf16[2,2,128,256]{3,2,1,0:T(8,128)(2,1)}, bf16[2,2,128,256]{3,2,1,0:T(8,128)(2,1)}) custom-call(bf16[4,1024,512]{2,1,0:T(8,128)(2,1)} %maximum_maximum_fusion.refs_0_, bf16[2,512,256]{2,1,0:T(8,128)(2,1)} %get-tuple-element.130.refs_1_, ...), custom_call_target="tpu_custom_call" | custom-call | flops 2147483648 | bytes 9437184 | tf_op jit(solution)/shard_map/own_beams/pallas_call | solution.py:211
  385.1 9.3 %spectrum.13 = (f32[2,128,1024]{2,1,0:T(8,128)}, f32[2048,128]{1,0:T(8,128)}) custom-call(s32[1]{0:T(128)} %bitcast.refs_0_, bf16[2,2,128,256]{3,2,1,0:T(8,128)(2,1)} %get-tuple-element.140.refs_9_.refs_1_, bf16[2,2,128,256]{3,2,1,0:T(8,128)(2,1)} %collective-permute-done.32.refs_2_, bf16[2,2,128,256]{3,2,1,0:T(8,128)(2,1)} %collective-permute-done.33.refs_3_, ...), custom_call_target="tpu_custom_call" | custom-call | flops 3221225472 | bytes 2097152 | tf_op jit(solution)/shard_map/spectrum/pallas_call | solution.py:319
  394.4 6.1 %collective-permute-start.42 = (bf16[2,2,128,256]{3,2,1,0:T(8,128)(2,1)}, bf16[2,2,128,256]{3,2,1,0:T(8,128)(2,1)}, u32[]{:S(2)}, u32[]{:S(2)}) collective-permute-start(bf16[2,2,128,256]{3,2,1,0:T(8,128)(2,1)} %get-tuple-element.156), channel_id=1, source_target_pairs={{0,2},{2,4},{4,6},{6,0},{1,3},{3,5},{5,7},{7,1},{8,10},{10,12},{12... | collective-permute-start | bytes 786440 | tf_op jit(solution)/shard_map/ppermute | solution.py:24
  413.2 6.2 %own_beams.15 = (bf16[2,2,128,256]{3,2,1,0:T(8,128)(2,1)}, bf16[2,2,128,256]{3,2,1,0:T(8,128)(2,1)}, bf16[2,2,128,256]{3,2,1,0:T(8,128)(2,1)}, bf16[2,2,128,256]{3,2,1,0:T(8,128)(2,1)}) custom-call(bf16[4,1024,512]{2,1,0:T(8,128)(2,1)} %maximum_maximum_fusion.refs_0_, bf16[2,512,256]{2,1,0:T(8,128)(2,1)} %get-tuple-element.149.refs_1_, ...), custom_call_target="tpu_custom_call" | custom-call | flops 2147483648 | bytes 9437184 | tf_op jit(solution)/shard_map/own_beams/pallas_call | solution.py:211
  421.9 9.4 %spectrum.14 = (f32[2,128,1024]{2,1,0:T(8,128)}, f32[2048,128]{1,0:T(8,128)}) custom-call(s32[1]{0:T(128)} %bitcast.refs_0_, bf16[2,2,128,256]{3,2,1,0:T(8,128)(2,1)} %get-tuple-element.154.refs_9_.refs_1_, bf16[2,2,128,256]{3,2,1,0:T(8,128)(2,1)} %collective-permute-done.42.refs_2_, bf16[2,2,128,256]{3,2,1,0:T(8,128)(2,1)} %collective-permute-done.43.refs_3_, ...), custom_call_target="tpu_custom_call" | custom-call | flops 3221225472 | bytes 2097152 | tf_op jit(solution)/shard_map/spectrum/pallas_call | solution.py:319
  449.0 9.2 %spectrum.15 = (f32[2,128,1024]{2,1,0:T(8,128)}, f32[2048,128]{1,0:T(8,128)}) custom-call(s32[1]{0:T(128)} %bitcast.refs_0_, bf16[2,2,128,256]{3,2,1,0:T(8,128)(2,1)} %get-tuple-element.164.refs_9_.refs_1_, bf16[2,2,128,256]{3,2,1,0:T(8,128)(2,1)} %copy-done.45, bf16[2,2,128,256]{3,2,1,0:T(8,128)(2,1)} %copy-done.48, bf16[2,2,128,256]{3,2,1,0:T(8,128)(2,1)} %copy-done.51, ...), custom_call_target="tpu_custom_call" | custom-call | flops 3221225472 | bytes 2097152 | tf_op jit(solution)/shard_map/spectrum/pallas_call | solution.py:319
  483.3 7.0 %place.2.refs_5_ = f32[128,16,1024]{2,1,0:T(8,128)} custom-call(f32[2,128,1024]{2,1,0:T(8,128)} %get-tuple-element.127.refs_5_.refs_0_, f32[2,128,1024]{2,1,0:T(8,128)} %get-tuple-element.129.refs_5_.refs_1_, f32[2,128,1024]{2,1,0:T(8,128)} %get-tuple-element.139.refs_5_.refs_2_, f32[2,128,1024]{2,1,0:T(8,128)} %get-tuple-element.153.refs_5_.refs_3_), custom_call_target="tpu_custom_call" | custom-call | tf_op jit(solution)/shard_map/place/pallas_call | solution.py:372
  490.3 6.9 %place.3 = f32[128,16,1024]{2,1,0:T(8,128)} custom-call(f32[2,128,1024]{2,1,0:T(8,128)} %get-tuple-element.155.refs_5_.refs_0_, f32[2,128,1024]{2,1,0:T(8,128)} %get-tuple-element.165.refs_5_.refs_1_, f32[2,128,1024]{2,1,0:T(8,128)} %get-tuple-element.174.refs_6_.refs_2_, ...), custom_call_target="tpu_custom_call", output_to_operand_aliasing={{}: (5, {})} | custom-call | tf_op jit(solution)/shard_map/place/pallas_call | solution.py:372
  (274 shorter events, 173.3 us)
Async XLA Ops:
  3.9 45.3 %collective-permute-start.7 = (bf16[2,512,256]{2,1,0:T(8,128)(2,1)}, bf16[2,512,256]{2,1,0:T(8,128)(2,1)}, u32[]{:S(2)}, u32[]{:S(2)}) collective-permute-start(bf16[2,512,256]{2,1,0:T(8,128)(2,1)} %get-tuple-element.97), channel_id=1, source_target_pairs={{0,24},{2,18},{4,28},{6,22},{8,16},{10,26},{12,20},{14,30},{16,8},... | collective-permute-start | bytes 1572872 | tf_op jit(solution)/shard_map/ppermute | solution.py:42
  12.1 37.6 %collective-permute-start.8 = (bf16[2,512,256]{2,1,0:T(8,128)(2,1)}, bf16[2,512,256]{2,1,0:T(8,128)(2,1)}, u32[]{:S(2)}, u32[]{:S(2)}) collective-permute-start(bf16[2,512,256]{2,1,0:T(8,128)(2,1)} %get-tuple-element.98), channel_id=1, source_target_pairs={{0,8},{2,26},{4,12},{6,30},{8,0},{10,18},{12,4},{14,22},{16,24},{1... | collective-permute-start | bytes 1572872 | tf_op jit(solution)/shard_map/ppermute | solution.py:42
  15.3 61.5 %collective-permute-start.6 = (bf16[2,512,256]{2,1,0:T(8,128)(2,1)}, bf16[2,512,256]{2,1,0:T(8,128)(2,1)}, u32[]{:S(2)}, u32[]{:S(2)}) collective-permute-start(bf16[2,512,256]{2,1,0:T(8,128)(2,1)} %get-tuple-element.96), channel_id=1, source_target_pairs={{0,16},{2,10},{4,20},{6,14},{8,24},{10,2},{12,28},{14,6},{16,0},{1... | collective-permute-start | bytes 1572872 | tf_op jit(solution)/shard_map/ppermute | solution.py:42
  15.8 68.2 %collective-permute-start.4 = (bf16[2,512,256]{2,1,0:T(8,128)(2,1)}, bf16[2,512,256]{2,1,0:T(8,128)(2,1)}, u32[]{:S(2)}, u32[]{:S(2)}) collective-permute-start(bf16[2,512,256]{2,1,0:T(8,128)(2,1)} %get-tuple-element.106), channel_id=1, source_target_pairs={{0,24},{2,18},{4,28},{6,22},{8,16},{10,26},{12,20},{14,30},{16,8},... | collective-permute-start | bytes 1572872 | tf_op jit(solution)/shard_map/ppermute | solution.py:42
  19.6 64.4 %collective-permute-start.5 = (bf16[2,512,256]{2,1,0:T(8,128)(2,1)}, bf16[2,512,256]{2,1,0:T(8,128)(2,1)}, u32[]{:S(2)}, u32[]{:S(2)}) collective-permute-start(bf16[2,512,256]{2,1,0:T(8,128)(2,1)} %get-tuple-element.107), channel_id=1, source_target_pairs={{0,8},{2,26},{4,12},{6,30},{8,0},{10,18},{12,4},{14,22},{16,24},{1... | collective-permute-start | bytes 1572872 | tf_op jit(solution)/shard_map/ppermute | solution.py:42
  49.2 49.6 %collective-permute-start.3 = (bf16[2,512,256]{2,1,0:T(8,128)(2,1)}, bf16[2,512,256]{2,1,0:T(8,128)(2,1)S(1)}, u32[]{:S(2)}, u32[]{:S(2)}) collective-permute-start(bf16[2,512,256]{2,1,0:T(8,128)(2,1)} %get-tuple-element.105), channel_id=1, source_target_pairs={{0,16},{2,10},{4,20},{6,14},{8,24},{10,2},{12,28},{14,6},{16,0},{1... | collective-permute-start | bytes 1572872 | tf_op jit(solution)/shard_map/ppermute | solution.py:42
  82.7 31.0 %collective-permute-start.13 = (bf16[2,1024,256]{2,1,0:T(8,128)(2,1)}, bf16[2,1024,256]{2,1,0:T(8,128)(2,1)}, u32[]{:S(2)}, u32[]{:S(2)}) collective-permute-start(bf16[2,1024,256]{2,1,0:T(8,128)(2,1)} %beam_partial.9.refs_5_), channel_id=1, source_target_pairs={{0,1},{1,0},{2,3},{3,2},{4,5},{5,4},{6,7},{7,6},{8,9},{9,8},{10,11... | collective-permute-start | bytes 3145736 | tf_op jit(solution)/shard_map/ppermute | solution.py:24
  105.6 78.6 %collective-permute-start.9 = (bf16[2,1024,256]{2,1,0:T(8,128)(2,1)}, bf16[2,1024,256]{2,1,0:T(8,128)(2,1)}, u32[]{:S(2)}, u32[]{:S(2)}) collective-permute-start(bf16[2,1024,256]{2,1,0:T(8,128)(2,1)} %beam_partial.10.refs_6_), channel_id=1, source_target_pairs={{0,1},{1,0},{2,3},{3,2},{4,5},{5,4},{6,7},{7,6},{8,9},{9,8},{10,11... | collective-permute-start | bytes 3145736 | tf_op jit(solution)/shard_map/ppermute | solution.py:24
  110.7 31.7 %collective-permute-start.12 = (bf16[2,512,256]{2,1,0:T(8,128)(2,1)}, bf16[2,512,256]{2,1,0:T(8,128)(2,1)}, u32[]{:S(2)}, u32[]{:S(2)}) collective-permute-start(bf16[2,512,256]{2,1,0:T(8,128)(2,1)} %get-tuple-element.113), channel_id=1, source_target_pairs={{0,8},{2,26},{4,12},{6,30},{8,0},{10,18},{12,4},{14,22},{16,24},{1... | collective-permute-start | bytes 1572872 | tf_op jit(solution)/shard_map/ppermute | solution.py:42
  110.7 62.3 %collective-permute-start.10 = (bf16[2,512,256]{2,1,0:T(8,128)(2,1)}, bf16[2,512,256]{2,1,0:T(8,128)(2,1)}, u32[]{:S(2)}, u32[]{:S(2)}) collective-permute-start(bf16[2,512,256]{2,1,0:T(8,128)(2,1)} %get-tuple-element.111), channel_id=1, source_target_pairs={{0,16},{2,10},{4,20},{6,14},{8,24},{10,2},{12,28},{14,6},{16,0},{1... | collective-permute-start | bytes 1572872 | tf_op jit(solution)/shard_map/ppermute | solution.py:42
  113.8 65.8 %collective-permute-start.22 = (bf16[2,512,256]{2,1,0:T(8,128)(2,1)}, bf16[2,512,256]{2,1,0:T(8,128)(2,1)S(1)}, u32[]{:S(2)}, u32[]{:S(2)}) collective-permute-start(bf16[2,512,256]{2,1,0:T(8,128)(2,1)} %get-tuple-element.125), channel_id=1, source_target_pairs={{0,24},{2,18},{4,28},{6,22},{8,16},{10,26},{12,20},{14,30},{16,8},... | collective-permute-start | bytes 1572872 | tf_op jit(solution)/shard_map/ppermute | solution.py:42
  124.3 61.5 %collective-permute-start.17 = (bf16[2,2,128,256]{3,2,1,0:T(8,128)(2,1)}, bf16[2,2,128,256]{3,2,1,0:T(8,128)(2,1)S(1)}, u32[]{:S(2)}, u32[]{:S(2)}) collective-permute-start(bf16[2,2,128,256]{3,2,1,0:T(8,128)(2,1)} %get-tuple-element.119), channel_id=1, source_target_pairs={{0,2},{2,4},{4,6},{6,0},{1,3},{3,5},{5,7},{7,1},{8,10},{10,12},{12... | collective-permute-start | bytes 786440 | tf_op jit(solution)/shard_map/ppermute | solution.py:24
  179.0 44.5 %collective-permute-start.20 = (bf16[2,1024,256]{2,1,0:T(8,128)(2,1)}, bf16[2,1024,256]{2,1,0:T(8,128)(2,1)}, u32[]{:S(2)}, u32[]{:S(2)}) collective-permute-start(bf16[2,1024,256]{2,1,0:T(8,128)(2,1)} %beam_partial.11.refs_6_), channel_id=1, source_target_pairs={{0,1},{1,0},{2,3},{3,2},{4,5},{5,4},{6,7},{7,6},{8,9},{9,8},{10,11... | collective-permute-start | bytes 3145736 | tf_op jit(solution)/shard_map/ppermute | solution.py:24
  179.5 26.1 %collective-permute-start.23 = (bf16[2,512,256]{2,1,0:T(8,128)(2,1)S(1)}, bf16[2,512,256]{2,1,0:T(8,128)(2,1)S(1)}, u32[]{:S(2)}, u32[]{:S(2)}) collective-permute-start(bf16[2,512,256]{2,1,0:T(8,128)(2,1)S(1)} %copy-done.29), channel_id=1, source_target_pairs={{0,8},{2,26},{4,12},{6,30},{8,0},{10,18},{12,4},{14,22},{16,24},{1... | collective-permute-start | bytes 1572872 | tf_op jit(solution)/shard_map/ppermute | solution.py:42
  179.6 27.5 %collective-permute-start.21 = (bf16[2,512,256]{2,1,0:T(8,128)(2,1)}, bf16[2,512,256]{2,1,0:T(8,128)(2,1)S(1)}, u32[]{:S(2)}, u32[]{:S(2)}) collective-permute-start(bf16[2,512,256]{2,1,0:T(8,128)(2,1)} %get-tuple-element.124), channel_id=1, source_target_pairs={{0,16},{2,10},{4,20},{6,14},{8,24},{10,2},{12,28},{14,6},{16,0},{1... | collective-permute-start | bytes 1572872 | tf_op jit(solution)/shard_map/ppermute | solution.py:42
  194.7 26.0 %collective-permute-start.14 = (bf16[2,2,128,256]{3,2,1,0:T(8,128)(2,1)}, bf16[2,2,128,256]{3,2,1,0:T(8,128)(2,1)S(1)}, u32[]{:S(2)}, u32[]{:S(2)}) collective-permute-start(bf16[2,2,128,256]{3,2,1,0:T(8,128)(2,1)} %get-tuple-element.116), channel_id=1, source_target_pairs={{0,2},{2,4},{4,6},{6,0},{1,3},{3,5},{5,7},{7,1},{8,10},{10,12},{12... | collective-permute-start | bytes 786440 | tf_op jit(solution)/shard_map/ppermute | solution.py:24
  194.7 28.8 %collective-permute-start.15 = (bf16[2,2,128,256]{3,2,1,0:T(8,128)(2,1)}, bf16[2,2,128,256]{3,2,1,0:T(8,128)(2,1)S(1)}, u32[]{:S(2)}, u32[]{:S(2)}) collective-permute-start(bf16[2,2,128,256]{3,2,1,0:T(8,128)(2,1)} %get-tuple-element.117), channel_id=1, source_target_pairs={{0,4},{2,6},{4,0},{6,2},{1,5},{3,7},{5,1},{7,3},{8,12},{10,14},{12... | collective-permute-start | bytes 786440 | tf_op jit(solution)/shard_map/ppermute | solution.py:24
  205.6 28.9 %collective-permute-start.16 = (bf16[2,2,128,256]{3,2,1,0:T(8,128)(2,1)S(1)}, bf16[2,2,128,256]{3,2,1,0:T(8,128)(2,1)}, u32[]{:S(2)}, u32[]{:S(2)}) collective-permute-start(bf16[2,2,128,256]{3,2,1,0:T(8,128)(2,1)S(1)} %copy-done.35), channel_id=1, source_target_pairs={{0,6},{2,0},{4,2},{6,4},{1,7},{3,1},{5,3},{7,5},{8,14},{10,8},{12,... | collective-permute-start | bytes 786440 | tf_op jit(solution)/shard_map/ppermute | solution.py:24
  213.8 77.5 %collective-permute-start.31 = (bf16[2,1024,256]{2,1,0:T(8,128)(2,1)}, bf16[2,1024,256]{2,1,0:T(8,128)(2,1)S(1)}, u32[]{:S(2)}, u32[]{:S(2)}) collective-permute-start(bf16[2,1024,256]{2,1,0:T(8,128)(2,1)} %beam_partial.12.refs_6_), channel_id=1, source_target_pairs={{0,1},{1,0},{2,3},{3,2},{4,5},{5,4},{6,7},{7,6},{8,9},{9,8},{10,11... | collective-permute-start | bytes 3145736 | tf_op jit(solution)/shard_map/ppermute | solution.py:24
  220.7 26.0 %collective-permute-start.1 = (bf16[2,512,256]{2,1,0:T(8,128)(2,1)}, bf16[2,512,256]{2,1,0:T(8,128)(2,1)S(1)}, u32[]{:S(2)}, u32[]{:S(2)}) collective-permute-start(bf16[2,512,256]{2,1,0:T(8,128)(2,1)} %get-tuple-element.102), channel_id=1, source_target_pairs={{0,24},{2,18},{4,28},{6,22},{8,16},{10,26},{12,20},{14,30},{16,8},... | collective-permute-start | bytes 1572872 | tf_op jit(solution)/shard_map/ppermute | solution.py:42
  223.5 29.8 %collective-permute-start.2 = (bf16[2,512,256]{2,1,0:T(8,128)(2,1)}, bf16[2,512,256]{2,1,0:T(8,128)(2,1)S(1)}, u32[]{:S(2)}, u32[]{:S(2)}) collective-permute-start(bf16[2,512,256]{2,1,0:T(8,128)(2,1)} %get-tuple-element.103), channel_id=1, source_target_pairs={{0,8},{2,26},{4,12},{6,30},{8,0},{10,18},{12,4},{14,22},{16,24},{1... | collective-permute-start | bytes 1572872 | tf_op jit(solution)/shard_map/ppermute | solution.py:42
  223.5 57.4 %collective-permute-start = (bf16[2,512,256]{2,1,0:T(8,128)(2,1)}, bf16[2,512,256]{2,1,0:T(8,128)(2,1)S(1)}, u32[]{:S(2)}, u32[]{:S(2)}) collective-permute-start(bf16[2,512,256]{2,1,0:T(8,128)(2,1)} %get-tuple-element.101), channel_id=1, source_target_pairs={{0,16},{2,10},{4,20},{6,14},{8,24},{10,2},{12,28},{14,6},{16,0},{1... | collective-permute-start | bytes 1572872 | tf_op jit(solution)/shard_map/ppermute | solution.py:42
  234.5 55.2 %collective-permute-start.26 = (bf16[2,512,256]{2,1,0:T(8,128)(2,1)}, bf16[2,512,256]{2,1,0:T(8,128)(2,1)S(1)}, u32[]{:S(2)}, u32[]{:S(2)}) collective-permute-start(bf16[2,512,256]{2,1,0:T(8,128)(2,1)} %get-tuple-element.132), channel_id=1, source_target_pairs={{0,24},{2,18},{4,28},{6,22},{8,16},{10,26},{12,20},{14,30},{16,8},... | collective-permute-start | bytes 1572872 | tf_op jit(solution)/shard_map/ppermute | solution.py:42
  287.7 38.0 %collective-permute-start.24 = (bf16[2,1024,256]{2,1,0:T(8,128)(2,1)}, bf16[2,1024,256]{2,1,0:T(8,128)(2,1)}, u32[]{:S(2)}, u32[]{:S(2)}) collective-permute-start(bf16[2,1024,256]{2,1,0:T(8,128)(2,1)} %beam_partial.13.refs_6_), channel_id=1, source_target_pairs={{0,1},{1,0},{2,3},{3,2},{4,5},{5,4},{6,7},{7,6},{8,9},{9,8},{10,11... | collective-permute-start | bytes 3145736 | tf_op jit(solution)/shard_map/ppermute | solution.py:24
  313.9 31.0 %collective-permute-start.40 = (bf16[2,512,256]{2,1,0:T(8,128)(2,1)}, bf16[2,512,256]{2,1,0:T(8,128)(2,1)S(1)}, u32[]{:S(2)}, u32[]{:S(2)}) collective-permute-start(bf16[2,512,256]{2,1,0:T(8,128)(2,1)} %get-tuple-element.151), channel_id=1, source_target_pairs={{0,24},{2,18},{4,28},{6,22},{8,16},{10,26},{12,20},{14,30},{16,8},... | collective-permute-start | bytes 1572872 | tf_op jit(solution)/shard_map/ppermute | solution.py:42
  317.7 29.5 %collective-permute-start.41 = (bf16[2,512,256]{2,1,0:T(8,128)(2,1)}, bf16[2,512,256]{2,1,0:T(8,128)(2,1)S(1)}, u32[]{:S(2)}, u32[]{:S(2)}) collective-permute-start(bf16[2,512,256]{2,1,0:T(8,128)(2,1)} %get-tuple-element.152), channel_id=1, source_target_pairs={{0,8},{2,26},{4,12},{6,30},{8,0},{10,18},{12,4},{14,22},{16,24},{1... | collective-permute-start | bytes 1572872 | tf_op jit(solution)/shard_map/ppermute | solution.py:42
  317.8 45.2 %collective-permute-start.39 = (bf16[2,512,256]{2,1,0:T(8,128)(2,1)}, bf16[2,512,256]{2,1,0:T(8,128)(2,1)S(1)}, u32[]{:S(2)}, u32[]{:S(2)}) collective-permute-start(bf16[2,512,256]{2,1,0:T(8,128)(2,1)} %get-tuple-element.150), channel_id=1, source_target_pairs={{0,16},{2,10},{4,20},{6,14},{8,24},{10,2},{12,28},{14,6},{16,0},{1... | collective-permute-start | bytes 1572872 | tf_op jit(solution)/shard_map/ppermute | solution.py:42
  325.7 47.7 %collective-permute-start.38 = (bf16[2,1024,256]{2,1,0:T(8,128)(2,1)}, bf16[2,1024,256]{2,1,0:T(8,128)(2,1)S(1)}, u32[]{:S(2)}, u32[]{:S(2)}) collective-permute-start(bf16[2,1024,256]{2,1,0:T(8,128)(2,1)} %beam_partial.14.refs_6_), channel_id=1, source_target_pairs={{0,1},{1,0},{2,3},{3,2},{4,5},{5,4},{6,7},{7,6},{8,9},{9,8},{10,11... | collective-permute-start | bytes 3145736 | tf_op jit(solution)/shard_map/ppermute | solution.py:24
  369.8 42.0 %collective-permute-start.45 = (bf16[2,1024,256]{2,1,0:T(8,128)(2,1)}, bf16[2,1024,256]{2,1,0:T(8,128)(2,1)S(1)}, u32[]{:S(2)}, u32[]{:S(2)}) collective-permute-start(bf16[2,1024,256]{2,1,0:T(8,128)(2,1)} %beam_partial.15.refs_6_), channel_id=1, source_target_pairs={{0,1},{1,0},{2,3},{3,2},{4,5},{5,4},{6,7},{7,6},{8,9},{9,8},{10,11... | collective-permute-start | bytes 3145736 | tf_op jit(solution)/shard_map/ppermute | solution.py:24
  373.5 59.4 %collective-permute-start.55 = (bf16[1,512,256]{2,1,0:T(8,128)(2,1)S(1)}, bf16[1,512,256]{2,1,0:T(8,128)(2,1)S(1)}, u32[]{:S(2)}, u32[]{:S(2)}) collective-permute-start(bf16[1,512,256]{2,1,0:T(8,128)(2,1)S(1)} %copy-done.30), channel_id=1, source_target_pairs={{0,8},{2,26},{4,12},{6,30},{8,0},{10,18},{12,4},{14,22},{16,24},{1... | collective-permute-start | bytes 786440 | tf_op jit(solution)/shard_map/ppermute | solution.py:42
  394.4 25.0 %collective-permute-start.42 = (bf16[2,2,128,256]{3,2,1,0:T(8,128)(2,1)}, bf16[2,2,128,256]{3,2,1,0:T(8,128)(2,1)}, u32[]{:S(2)}, u32[]{:S(2)}) collective-permute-start(bf16[2,2,128,256]{3,2,1,0:T(8,128)(2,1)} %get-tuple-element.156), channel_id=1, source_target_pairs={{0,2},{2,4},{4,6},{6,0},{1,3},{3,5},{5,7},{7,1},{8,10},{10,12},{12... | collective-permute-start | bytes 786440 | tf_op jit(solution)/shard_map/ppermute | solution.py:24
  421.7 23.7 %collective-permute-start.49 = (bf16[2,2,128,256]{3,2,1,0:T(8,128)(2,1)}, bf16[2,2,128,256]{3,2,1,0:T(8,128)(2,1)S(1)}, u32[]{:S(2)}, u32[]{:S(2)}) collective-permute-start(bf16[2,2,128,256]{3,2,1,0:T(8,128)(2,1)} %get-tuple-element.166), channel_id=1, source_target_pairs={{0,2},{2,4},{4,6},{6,0},{1,3},{3,5},{5,7},{7,1},{8,10},{10,12},{12... | collective-permute-start | bytes 786440 | tf_op jit(solution)/shard_map/ppermute | solution.py:24
  (92 other events, 921.2 us)
where the time goes:
time: 507 us; the launch traced here: 498 us
  Pallas kernels  219 us (43%)
  waiting for transfers between devices  138 us (27%)
  starting transfers between devices  100 us (20%)
  other arithmetic  25.5 us (5%)
  local copies, waits for them, and re-layouts  13.5 us (3%)
    ppermute x27, waiting for transfers between devices, exchange(): return lax.ppermute(value, ('channel', 'tm'), pairs)  131 us
    pallas_call x9, Pallas kernels, spectrum(): pl.pallas_call(functools.partial(spectrum_kernel, len(blocks), trial_bloc...  76.7 us
    ppermute x39, starting transfers between devices, ring(): lax.ppermute(value, axis, [(i, (i + shift) % count) for i in range(count)])  58.8 us
    pallas_call x9, Pallas kernels, own_beams(): pl.pallas_call(functools.partial(own_kernel, len(pieces), len(received)),...  52.6 us
    pallas_call x9, Pallas kernels, beam_partial(): pl.pallas_call(partial_kernel, grid=(chans,), in_specs=[pl.BlockSpec((sou...  50.8 us
    ppermute x27, starting transfers between devices, exchange(): return lax.ppermute(value, ('channel', 'tm'), pairs)  41.7 us
    pallas_call x8, Pallas kernels, spread(): pl.pallas_call(spread_kernel, grid_spec=pltpu.PrefetchScalarGridSpec(num_...  25.3 us
    pallas_call x2, Pallas kernels, place(): pl.pallas_call(functools.partial(place_kernel, len(chunks)), grid=(beams...  13.9 us
  transfers between devices with their start and end apart: 66, of which 11 were waited for; matrix products, arithmetic and copies ran while one was open for 6% of the time, Pallas kernels for 42%

commit v1 on v0

--- a/solution.py
+++ b/solution.py
@@ -100,7 +100,7 @@
 def frame_distance(frames):
     row = np.arange(frames)[:, None]
     col = np.arange(frames * UPCH)[None, :] // UPCH
-    return ((row - col) % frames).astype(np.int32)
+    return ((row - col) % frames).astype(jnp.bfloat16)
 
 
 def spread_kernel(index_ref, v_ref, order_ref, *out_refs):
@@ -283,9 +283,10 @@
             dist = dist_ref[:, lanes]
             for d in range(trial_block):
                 wanted = delay_ref[pl.ds(g * trial_block + d, 1), :]
+                wanted = jnp.broadcast_to(wanted, dist.shape).astype(jnp.bfloat16)
                 hot_ref[d * frames : (d + 1) * frames, lanes] = jnp.where(
-                    dist == wanted, 1.0, 0.0
-                ).astype(jnp.bfloat16)
+                    dist == wanted, jnp.bfloat16(1.0), jnp.bfloat16(0.0)
+                )
         rows = pl.ds(pl.multiple_of(g * (trial_block * frames), trial_block * frames), trial_block * frames)
         acc_ref[rows, :] += lax.dot_general(
             hot_ref[...], c_ref[...], (((1,), (1,)), ((), ())), preferred_element_type=jnp.float32
@@ -382,12 +383,9 @@
 
 
 def chunk_sizes(count):
-    eighth = count // 8
-    if not eighth:
-        return [1] * count
-    rest = count - 7 * eighth
-    small = max(1, rest // 2)
-    return [eighth] * 7 + [rest - small, small]
+    eighth = max(1, count // 8)
+    sizes = [eighth] * (count // eighth)
+    return sizes + [count - sum(sizes)] if sum(sizes) < count else sizes
 
 
 def grouped_sizes(sizes, block):
@@ -471,10 +469,10 @@
     trial_order = (my_chan + jnp.arange(n_chan)) % n_chan
     delay_rows = delays.reshape(n_chan, trials // n_chan, own_channels, UPCH)[trial_order]
     delay_rows = jnp.transpose(delay_rows, (2, 0, 1, 3)).reshape(own_channels, trials, UPCH)
-    delay_rows = jnp.tile(delay_rows, (1, 1, LANES // UPCH))
+    delay_rows = jnp.tile(delay_rows, (1, 1, LANES // UPCH)).astype(jnp.float32)
     me = my_time.astype(jnp.int32).reshape(1)
 
-    powers = []
+    powers, held, placed = [], [], 0
     sums = jnp.zeros((trials * frames, own_count), jnp.float32)
     received, blocks = {}, {}
     last = len(pieces) - 1
@@ -509,6 +507,11 @@
             powers.append(power)
             sums = out_sums[0]
             token = power
+            if groups is not None and index < last and len(powers) == len(groups[placed]):
+                held = [place(powers, placed, own_channels, held)]
+                token = held[0]
+                powers = []
+                placed += 1
     total = sums
     for s in range(1, n_chan):
         total = total + ring(out_sums[s], "channel", s).astype(jnp.float32)
@@ -519,11 +522,7 @@
     if groups is None:
         intensity = jnp.transpose(jnp.concatenate(powers, axis=0), (1, 0, 2))
     else:
-        held = []
-        for g, group in enumerate(groups):
-            held = [place(powers[: len(group)], g, own_channels, held)]
-            powers = powers[len(group) :]
-        intensity = held[0]
+        intensity = place(powers, placed, own_channels, held)
     return (intensity, dedispersed)
 
 

time: 507 us -> 486 us (0.959)
  waiting for transfers between devices: 138 us -> 94.5 us
  starting transfers between devices: 100 us -> 135 us
  Pallas kernels: 219 us -> 211 us
    ppermute x27 -> x24, waiting for transfers between devices: 131 us -> 82.7 us  [exchange(): return lax.ppermute(value, ('channel', 'tm'), pairs)]
    ppermute x27 -> x24, starting transfers between devices: 41.7 us -> 74.5 us  [exchange(): return lax.ppermute(value, ('channel', 'tm'), pairs)]
    ppermute x39 -> x35, waiting for transfers between devices: 6.98 us -> 11.8 us  [ring(): lax.ppermute(value, axis, [(i, (i + shift) % count) for i in range(count)])]
    pallas_call x9 -> x8, Pallas kernels: 52.6 us -> 49.5 us  [own_beams(): pl.pallas_call(functools.partial(own_kernel, len(pieces), len(received)),...]
    pallas_call x9 -> x8, Pallas kernels: 50.8 us -> 47.9 us  [beam_partial(): pl.pallas_call(partial_kernel, grid=(chans,), in_specs=[pl.BlockSpec((sou...]
    pallas_call x9 -> x8, Pallas kernels: 76.7 us -> 73.7 us  [spectrum(): pl.pallas_call(functools.partial(spectrum_kernel, len(blocks), trial_bloc...]
    ppermute x39 -> x35, starting transfers between devices: 58.8 us -> 60.5 us  [ring(): lax.ppermute(value, axis, [(i, (i + shift) % count) for i in range(count)])]
  transfers between devices with their start and end apart: 66 -> 59, of which waited for: 11 -> 11; matrix products, arithmetic and copies ran while one was open for 6% -> 5% of each run, Pallas kernels for 42% -> 42%
where the time goes in v1:
time: 486 us; the launch traced here: 478 us
  Pallas kernels  211 us (43%)
  starting transfers between devices  135 us (28%)
  waiting for transfers between devices  94.5 us (19%)
  other arithmetic  22.9 us (5%)
  local copies, waits for them, and re-layouts  13.1 us (3%)
    ppermute x24, waiting for transfers between devices, exchange(): return lax.ppermute(value, ('channel', 'tm'), pairs)  82.7 us
    ppermute x24, starting transfers between devices, exchange(): return lax.ppermute(value, ('channel', 'tm'), pairs)  74.5 us
    pallas_call x8, Pallas kernels, spectrum(): pl.pallas_call(functools.partial(spectrum_kernel, len(blocks), trial_bloc...  73.7 us
    ppermute x35, starting transfers between devices, ring(): lax.ppermute(value, axis, [(i, (i + shift) % count) for i in range(count)])  60.5 us
    pallas_call x8, Pallas kernels, own_beams(): pl.pallas_call(functools.partial(own_kernel, len(pieces), len(received)),...  49.5 us
    pallas_call x8, Pallas kernels, beam_partial(): pl.pallas_call(partial_kernel, grid=(chans,), in_specs=[pl.BlockSpec((sou...  47.9 us
    pallas_call x8, Pallas kernels, spread(): pl.pallas_call(spread_kernel, grid_spec=pltpu.PrefetchScalarGridSpec(num_...  25.5 us
    pallas_call x2, Pallas kernels, place(): pl.pallas_call(functools.partial(place_kernel, len(chunks)), grid=(beams...  14.2 us
  transfers between devices with their start and end apart: 59, of which 11 were waited for; matrix products, arithmetic and copies ran while one was open for 5% of the time, Pallas kernels for 42%

profile of v1, /device:TPU:0, one launch (start us, length us, event | category | flops | bytes accessed | tf_op | source)
XLA Modules:
  0.0 477.8 jit_solution(12514716429930134229)
XLA Ops:
  19.9 9.1 %multiply_convert_fusion = (bf16[4,512,256]{2,1,0:T(8,128)(2,1)S(1)}, bf16[4,512,256]{2,1,0:T(8,128)(2,1)S(1)}, bf16[4,512,256]{2,1,0:T(8,128)(2,1)S(1)}, bf16[4,512,256]{2,1,0:T(8,128)(2,1)S(1)}) fusion(s32[512]{0:T(512)S(1)} %get-tuple-element.183, s32[512]{0:T(512)S(1)} %get-tuple-element.180, s32[4,256]{1,0:T(4,128)S(1)} %get-tuple-element.179, ...), kind=kLoop, calls=%fused_computation.14 | loop fusion | flops 63963136 | bytes 4210688 | tf_op jit(solution)/shard_map/convert_element_type | solution.py:69
  29.0 8.4 %fusion.27 = (bf16[4,512,256]{2,1,0:T(8,128)(2,1)S(1)}, bf16[4,512,256]{2,1,0:T(8,128)(2,1)S(1)}) fusion(s32[4,256]{1,0:T(4,128)S(1)} %get-tuple-element.179, s32[512]{0:T(512)S(1)} %get-tuple-element.183, s32[4,256]{1,0:T(4,128)S(1)} %get-tuple-element.178, s32[512]{0:T(512)S(1)} %get-tuple-element.180, s32[512]{0:T(512)S(1)} %get-tuple-element.182, ...), kind=kLoop, calls=%fused_computation.97 | loop fusion | flops 59768832 | bytes 2113536 | tf_op jit(solution)/shard_map/neg | solution.py:460
  37.4 48.6 %collective-permute-done.6.refs_2_ = bf16[2,512,256]{2,1,0:T(8,128)(2,1)} collective-permute-done((bf16[2,512,256]{2,1,0:T(8,128)(2,1)}, bf16[2,512,256]{2,1,0:T(8,128)(2,1)}, u32[]{:S(2)}, u32[]{:S(2)}) %collective-permute-start.6) | collective-permute-done | bytes 524320 | tf_op jit(solution)/shard_map/ppermute | solution.py:42
  104.4 6.0 %beam_partial.9.refs_6_ = bf16[2,1024,256]{2,1,0:T(8,128)(2,1)} custom-call(bf16[4,1024,512]{2,1,0:T(8,128)(2,1)} %maximum_maximum_fusion.1.refs_0_, bf16[2,512,256]{2,1,0:T(8,128)(2,1)} %get-tuple-element.94.refs_1_, bf16[2,512,256]{2,1,0:T(8,128)(2,1)} %collective-permute-done.3.refs_2_, bf16[2,512,256]{2,1,0:T(8,128)(2,1)} %collective-permute-done.4.refs_3_, ...), custom_call_target="tpu_custom_call" | custom-call | flops 2147483648 | bytes 7340032 | tf_op jit(solution)/shard_map/beam_partial/pallas_call | solution.py:168
  122.4 6.2 %own_beams.8 = (bf16[2,2,128,256]{3,2,1,0:T(8,128)(2,1)}, bf16[2,2,128,256]{3,2,1,0:T(8,128)(2,1)}, bf16[2,2,128,256]{3,2,1,0:T(8,128)(2,1)}, bf16[2,2,128,256]{3,2,1,0:T(8,128)(2,1)}) custom-call(bf16[4,1024,512]{2,1,0:T(8,128)(2,1)} %maximum_maximum_fusion.refs_0_, bf16[2,512,256]{2,1,0:T(8,128)(2,1)} %get-tuple-element.98.refs_1_, ...), custom_call_target="tpu_custom_call" | custom-call | flops 2147483648 | bytes 9437184 | tf_op jit(solution)/shard_map/own_beams/pallas_call | solution.py:211
  132.4 18.7 %collective-permute-done.10.refs_2_ = bf16[2,512,256]{2,1,0:T(8,128)(2,1)} collective-permute-done((bf16[2,512,256]{2,1,0:T(8,128)(2,1)}, bf16[2,512,256]{2,1,0:T(8,128)(2,1)}, u32[]{:S(2)}, u32[]{:S(2)}) %collective-permute-start.10) | collective-permute-done | bytes 524320 | tf_op jit(solution)/shard_map/ppermute | solution.py:42
  154.4 18.7 %collective-permute-start.21 = (bf16[2,512,256]{2,1,0:T(8,128)(2,1)S(1)}, bf16[2,512,256]{2,1,0:T(8,128)(2,1)S(1)}, u32[]{:S(2)}, u32[]{:S(2)}) collective-permute-start(bf16[2,512,256]{2,1,0:T(8,128)(2,1)S(1)} %copy-done.20), channel_id=1, source_target_pairs={{0,16},{2,10},{4,20},{6,14},{8,24},{10,2},{12,28},{14,6},{16,0},{1... | collective-permute-start | bytes 1572872 | tf_op jit(solution)/shard_map/ppermute | solution.py:42
  173.8 6.0 %beam_partial.10.refs_6_ = bf16[2,1024,256]{2,1,0:T(8,128)(2,1)} custom-call(bf16[4,1024,512]{2,1,0:T(8,128)(2,1)} %maximum_maximum_fusion.1.refs_0_, bf16[2,512,256]{2,1,0:T(8,128)(2,1)} %get-tuple-element.100.refs_1_, bf16[2,512,256]{2,1,0:T(8,128)(2,1)} %collective-permute-done.10.refs_2_, bf16[2,512,256]{2,1,0:T(8,128)(2,1)} %collective-permute-done.11.refs_3_, ...), custom_call_target="tpu_custom_call" | custom-call | flops 2147483648 | bytes 7340032 | tf_op jit(solution)/shard_map/beam_partial/pallas_call | solution.py:168
  180.5 6.2 %own_beams.9 = (bf16[2,2,128,256]{3,2,1,0:T(8,128)(2,1)}, bf16[2,2,128,256]{3,2,1,0:T(8,128)(2,1)}, bf16[2,2,128,256]{3,2,1,0:T(8,128)(2,1)}, bf16[2,2,128,256]{3,2,1,0:T(8,128)(2,1)}) custom-call(bf16[4,1024,512]{2,1,0:T(8,128)(2,1)} %maximum_maximum_fusion.refs_0_, bf16[2,512,256]{2,1,0:T(8,128)(2,1)} %get-tuple-element.94.refs_1_, ...), custom_call_target="tpu_custom_call" | custom-call | flops 2147483648 | bytes 9437184 | tf_op jit(solution)/shard_map/own_beams/pallas_call | solution.py:211
  192.2 9.2 %spectrum.8 = (f32[2,128,1024]{2,1,0:T(8,128)}, f32[2048,128]{1,0:T(8,128)}) custom-call(s32[1]{0:T(128)} %bitcast.refs_0_, bf16[2,2,128,256]{3,2,1,0:T(8,128)(2,1)} %get-tuple-element.104.refs_5_.refs_1_, bf16[2,2,128,256]{3,2,1,0:T(8,128)(2,1)} %copy-done.24, bf16[2,2,128,256]{3,2,1,0:T(8,128)(2,1)} %collective-permute-done.18.refs_3_, ...), custom_call_target="tpu_custom_call" | custom-call | flops 3221225472 | bytes 2097152 | tf_op jit(solution)/shard_map/spectrum/pallas_call | solution.py:320
  202.5 6.0 %beam_partial.11.refs_6_ = bf16[2,1024,256]{2,1,0:T(8,128)(2,1)} custom-call(bf16[4,1024,512]{2,1,0:T(8,128)(2,1)} %maximum_maximum_fusion.1.refs_0_, bf16[2,512,256]{2,1,0:T(8,128)(2,1)} %get-tuple-element.113.refs_1_, bf16[2,512,256]{2,1,0:T(8,128)(2,1)} %copy-done.1, bf16[2,512,256]{2,1,0:T(8,128)(2,1)} %copy-done.3, bf16[2,512,256]{2,1,0:T(8,128)(2,1)} %copy-done.5, ...), custom_call_target="tpu_custom_call" | custom-call | flops 2147483648 | bytes 7340032 | tf_op jit(solution)/shard_map/beam_partial/pallas_call | solution.py:168
  228.4 6.2 %own_beams.10 = (bf16[2,2,128,256]{3,2,1,0:T(8,128)(2,1)}, bf16[2,2,128,256]{3,2,1,0:T(8,128)(2,1)}, bf16[2,2,128,256]{3,2,1,0:T(8,128)(2,1)}, bf16[2,2,128,256]{3,2,1,0:T(8,128)(2,1)}) custom-call(bf16[4,1024,512]{2,1,0:T(8,128)(2,1)} %maximum_maximum_fusion.refs_0_, bf16[2,512,256]{2,1,0:T(8,128)(2,1)} %get-tuple-element.100.refs_1_, ...), custom_call_target="tpu_custom_call" | custom-call | flops 2147483648 | bytes 9437184 | tf_op jit(solution)/shard_map/own_beams/pallas_call | solution.py:211
  236.3 9.2 %spectrum.9 = (f32[2,128,1024]{2,1,0:T(8,128)}, f32[2048,128]{1,0:T(8,128)}) custom-call(s32[1]{0:T(128)} %bitcast.refs_0_, bf16[2,2,128,256]{3,2,1,0:T(8,128)(2,1)} %get-tuple-element.105.refs_9_.refs_1_, bf16[2,2,128,256]{3,2,1,0:T(8,128)(2,1)} %copy-done.30, bf16[2,2,128,256]{3,2,1,0:T(8,128)(2,1)} %copy-done.32, bf16[2,2,128,256]{3,2,1,0:T(8,128)(2,1)} %copy-done.37, ...), custom_call_target="tpu_custom_call" | custom-call | flops 3221225472 | bytes 2097152 | tf_op jit(solution)/shard_map/spectrum/pallas_call | solution.py:320
  245.6 6.6 %collective-permute-start.25 = (bf16[2,512,256]{2,1,0:T(8,128)(2,1)}, bf16[2,512,256]{2,1,0:T(8,128)(2,1)S(1)}, u32[]{:S(2)}, u32[]{:S(2)}) collective-permute-start(bf16[2,512,256]{2,1,0:T(8,128)(2,1)} %get-tuple-element.121), channel_id=1, source_target_pairs={{0,16},{2,10},{4,20},{6,14},{8,24},{10,2},{12,28},{14,6},{16,0},{1... | collective-permute-start | bytes 1572872 | tf_op jit(solution)/shard_map/ppermute | solution.py:42
  254.5 20.8 %collective-permute-start.30 = (bf16[2,2,128,256]{3,2,1,0:T(8,128)(2,1)S(1)}, bf16[2,2,128,256]{3,2,1,0:T(8,128)(2,1)}, u32[]{:S(2)}, u32[]{:S(2)}) collective-permute-start(bf16[2,2,128,256]{3,2,1,0:T(8,128)(2,1)S(1)} %copy-done.28), channel_id=1, source_target_pairs={{0,6},{2,0},{4,2},{6,4},{1,7},{3,1},{5,3},{7,5},{8,14},{10,8},{12,... | collective-permute-start | bytes 786440 | tf_op jit(solution)/shard_map/ppermute | solution.py:24
  281.9 6.2 %own_beams.11 = (bf16[2,2,128,256]{3,2,1,0:T(8,128)(2,1)}, bf16[2,2,128,256]{3,2,1,0:T(8,128)(2,1)}, bf16[2,2,128,256]{3,2,1,0:T(8,128)(2,1)}, bf16[2,2,128,256]{3,2,1,0:T(8,128)(2,1)}) custom-call(bf16[4,1024,512]{2,1,0:T(8,128)(2,1)} %maximum_maximum_fusion.refs_0_, bf16[2,512,256]{2,1,0:T(8,128)(2,1)} %get-tuple-element.113.refs_1_, ...), custom_call_target="tpu_custom_call" | custom-call | flops 2147483648 | bytes 9437184 | tf_op jit(solution)/shard_map/own_beams/pallas_call | solution.py:211
  288.2 9.3 %spectrum.10 = (f32[2,128,1024]{2,1,0:T(8,128)}, f32[2048,128]{1,0:T(8,128)}) custom-call(s32[1]{0:T(128)} %bitcast.refs_0_, bf16[2,2,128,256]{3,2,1,0:T(8,128)(2,1)} %get-tuple-element.118.refs_9_.refs_1_, bf16[2,2,128,256]{3,2,1,0:T(8,128)(2,1)} %copy-done.29, bf16[2,2,128,256]{3,2,1,0:T(8,128)(2,1)} %copy-done.33, ...), custom_call_target="tpu_custom_call" | custom-call | flops 3221225472 | bytes 2097152 | tf_op jit(solution)/shard_map/spectrum/pallas_call | solution.py:320
  298.7 6.0 %beam_partial.13.refs_6_ = bf16[2,1024,256]{2,1,0:T(8,128)(2,1)} custom-call(bf16[4,1024,512]{2,1,0:T(8,128)(2,1)} %maximum_maximum_fusion.1.refs_0_, bf16[2,512,256]{2,1,0:T(8,128)(2,1)} %get-tuple-element.120.refs_1_, bf16[2,512,256]{2,1,0:T(8,128)(2,1)} %copy-done.4, bf16[2,512,256]{2,1,0:T(8,128)(2,1)} %copy-done.6, bf16[2,512,256]{2,1,0:T(8,128)(2,1)} %copy-done.7, ...), custom_call_target="tpu_custom_call" | custom-call | flops 2147483648 | bytes 7340032 | tf_op jit(solution)/shard_map/beam_partial/pallas_call | solution.py:168
  317.8 10.7 %collective-permute-start.41 = (bf16[2,512,256]{2,1,0:T(8,128)(2,1)}, bf16[2,512,256]{2,1,0:T(8,128)(2,1)S(1)}, u32[]{:S(2)}, u32[]{:S(2)}) collective-permute-start(bf16[2,512,256]{2,1,0:T(8,128)(2,1)} %get-tuple-element.142), channel_id=1, source_target_pairs={{0,8},{2,26},{4,12},{6,30},{8,0},{10,18},{12,4},{14,22},{16,24},{1... | collective-permute-start | bytes 1572872 | tf_op jit(solution)/shard_map/ppermute | solution.py:42
  328.4 6.2 %own_beams.12 = (bf16[2,2,128,256]{3,2,1,0:T(8,128)(2,1)}, bf16[2,2,128,256]{3,2,1,0:T(8,128)(2,1)}, bf16[2,2,128,256]{3,2,1,0:T(8,128)(2,1)}, bf16[2,2,128,256]{3,2,1,0:T(8,128)(2,1)}) custom-call(bf16[4,1024,512]{2,1,0:T(8,128)(2,1)} %maximum_maximum_fusion.refs_0_, bf16[2,512,256]{2,1,0:T(8,128)(2,1)} %get-tuple-element.90.refs_1_, ...), custom_call_target="tpu_custom_call" | custom-call | flops 2147483648 | bytes 9437184 | tf_op jit(solution)/shard_map/own_beams/pallas_call | solution.py:211
  335.3 9.2 %spectrum.11 = (f32[2,128,1024]{2,1,0:T(8,128)}, f32[2048,128]{1,0:T(8,128)}) custom-call(s32[1]{0:T(128)} %bitcast.refs_0_, bf16[2,2,128,256]{3,2,1,0:T(8,128)(2,1)} %get-tuple-element.128.refs_9_.refs_1_, bf16[2,2,128,256]{3,2,1,0:T(8,128)(2,1)} %copy-done.39, bf16[2,2,128,256]{3,2,1,0:T(8,128)(2,1)} %copy-done.41, ...), custom_call_target="tpu_custom_call" | custom-call | flops 3221225472 | bytes 2097152 | tf_op jit(solution)/shard_map/spectrum/pallas_call | solution.py:320
  344.5 7.1 %place.2.refs_5_.refs_4_ = f32[128,16,1024]{2,1,0:T(8,128)} custom-call(f32[2,128,1024]{2,1,0:T(8,128)} %get-tuple-element.117.refs_5_.refs_0_, f32[2,128,1024]{2,1,0:T(8,128)} %get-tuple-element.119.refs_5_.refs_1_, f32[2,128,1024]{2,1,0:T(8,128)} %get-tuple-element.129.refs_5_.refs_2_, f32[2,128,1024]{2,1,0:T(8,128)} %get-tuple-element.143.refs_3_), custom_call_target="tpu_custom_call" | custom-call | tf_op jit(solution)/shard_map/place/pallas_call | solution.py:373
  364.6 6.2 %own_beams.13 = (bf16[2,2,128,256]{3,2,1,0:T(8,128)(2,1)}, bf16[2,2,128,256]{3,2,1,0:T(8,128)(2,1)}, bf16[2,2,128,256]{3,2,1,0:T(8,128)(2,1)}, bf16[2,2,128,256]{3,2,1,0:T(8,128)(2,1)}) custom-call(bf16[4,1024,512]{2,1,0:T(8,128)(2,1)} %maximum_maximum_fusion.refs_0_, bf16[2,512,256]{2,1,0:T(8,128)(2,1)} %get-tuple-element.120.refs_1_, ...), custom_call_target="tpu_custom_call" | custom-call | flops 2147483648 | bytes 9437184 | tf_op jit(solution)/shard_map/own_beams/pallas_call | solution.py:211
  371.5 9.2 %spectrum.12 = (f32[2,128,1024]{2,1,0:T(8,128)}, f32[2048,128]{1,0:T(8,128)}) custom-call(s32[1]{0:T(128)} %bitcast.refs_0_, bf16[2,2,128,256]{3,2,1,0:T(8,128)(2,1)} %get-tuple-element.130.refs_9_.refs_1_, bf16[2,2,128,256]{3,2,1,0:T(8,128)(2,1)} %collective-permute-done.32.refs_2_, bf16[2,2,128,256]{3,2,1,0:T(8,128)(2,1)} %collective-permute-done.33.refs_3_, ...), custom_call_target="tpu_custom_call" | custom-call | flops 3221225472 | bytes 2097152 | tf_op jit(solution)/shard_map/spectrum/pallas_call | solution.py:320
  380.7 9.5 %collective-permute-done.46.refs_2_ = bf16[2,512,256]{2,1,0:T(8,128)(2,1)S(1)} collective-permute-done((bf16[2,512,256]{2,1,0:T(8,128)(2,1)}, bf16[2,512,256]{2,1,0:T(8,128)(2,1)S(1)}, u32[]{:S(2)}, u32[]{:S(2)}) %collective-permute-start.46) | collective-permute-done | bytes 524320 | tf_op jit(solution)/shard_map/ppermute | solution.py:42
  398.0 8.4 %collective-permute-start.42 = (bf16[2,2,128,256]{3,2,1,0:T(8,128)(2,1)S(1)}, bf16[2,2,128,256]{3,2,1,0:T(8,128)(2,1)S(1)}, u32[]{:S(2)}, u32[]{:S(2)}) collective-permute-start(bf16[2,2,128,256]{3,2,1,0:T(8,128)(2,1)S(1)} %copy-done.35), channel_id=1, source_target_pairs={{0,2},{2,4},{4,6},{6,0},{1,3},{3,5},{5,7},{7,1},{8,10},{10,12},{12... | collective-permute-start | bytes 786440 | tf_op jit(solution)/shard_map/ppermute | solution.py:24
  408.0 6.2 %own_beams.14 = (bf16[2,2,128,256]{3,2,1,0:T(8,128)(2,1)}, bf16[2,2,128,256]{3,2,1,0:T(8,128)(2,1)}, bf16[2,2,128,256]{3,2,1,0:T(8,128)(2,1)}, bf16[2,2,128,256]{3,2,1,0:T(8,128)(2,1)}) custom-call(bf16[4,1024,512]{2,1,0:T(8,128)(2,1)} %maximum_maximum_fusion.refs_0_, bf16[2,512,256]{2,1,0:T(8,128)(2,1)} %get-tuple-element.139.refs_1_, ...), custom_call_target="tpu_custom_call" | custom-call | flops 2147483648 | bytes 9437184 | tf_op jit(solution)/shard_map/own_beams/pallas_call | solution.py:211
  420.5 9.3 %spectrum.13 = (f32[2,128,1024]{2,1,0:T(8,128)}, f32[2048,128]{1,0:T(8,128)}) custom-call(s32[1]{0:T(128)} %bitcast.refs_0_, bf16[2,2,128,256]{3,2,1,0:T(8,128)(2,1)} %get-tuple-element.144.refs_9_.refs_1_, bf16[2,2,128,256]{3,2,1,0:T(8,128)(2,1)} %copy-done.42, bf16[2,2,128,256]{3,2,1,0:T(8,128)(2,1)} %copy-done.44, bf16[2,2,128,256]{3,2,1,0:T(8,128)(2,1)} %copy-done.46, ...), custom_call_target="tpu_custom_call" | custom-call | flops 3221225472 | bytes 2097152 | tf_op jit(solution)/shard_map/spectrum/pallas_call | solution.py:320
  430.8 6.2 %own_beams.15 = (bf16[2,2,128,256]{3,2,1,0:T(8,128)(2,1)}, bf16[2,2,128,256]{3,2,1,0:T(8,128)(2,1)}, bf16[2,2,128,256]{3,2,1,0:T(8,128)(2,1)}, bf16[2,2,128,256]{3,2,1,0:T(8,128)(2,1)}) custom-call(bf16[4,1024,512]{2,1,0:T(8,128)(2,1)} %maximum_maximum_fusion.refs_0_, bf16[2,512,256]{2,1,0:T(8,128)(2,1)} %get-tuple-element.150.refs_1_, ...), custom_call_target="tpu_custom_call" | custom-call | flops 2147483648 | bytes 9437184 | tf_op jit(solution)/shard_map/own_beams/pallas_call | solution.py:211
  440.8 9.3 %spectrum.14 = (f32[2,128,1024]{2,1,0:T(8,128)}, f32[2048,128]{1,0:T(8,128)}) custom-call(s32[1]{0:T(128)} %bitcast.refs_0_, bf16[2,2,128,256]{3,2,1,0:T(8,128)(2,1)} %get-tuple-element.153.refs_9_.refs_1_, bf16[2,2,128,256]{3,2,1,0:T(8,128)(2,1)} %copy-done.34, bf16[2,2,128,256]{3,2,1,0:T(8,128)(2,1)} %copy-done.38, bf16[2,2,128,256]{3,2,1,0:T(8,128)(2,1)} %copy-done.40, ...), custom_call_target="tpu_custom_call" | custom-call | flops 3221225472 | bytes 2097152 | tf_op jit(solution)/shard_map/spectrum/pallas_call | solution.py:320
  451.2 9.1 %spectrum.15 = (f32[2,128,1024]{2,1,0:T(8,128)}, f32[512,128]{1,0:T(8,128)}, bf16[512,128]{1,0:T(8,128)(2,1)}, bf16[512,128]{1,0:T(8,128)(2,1)}, bf16[512,128]{1,0:T(8,128)(2,1)}) custom-call(s32[1]{0:T(128)} %bitcast.refs_0_, bf16[2,2,128,256]{3,2,1,0:T(8,128)(2,1)} %get-tuple-element.159.refs_9_.refs_1_, bf16[2,2,128,256]{3,2,1,0:T(8,128)(2,1)} %copy-done.43, ...), custom_call_target="tpu_custom_call" | custom-call | flops 3221225472 | bytes 2097152 | tf_op jit(solution)/shard_map/spectrum/pallas_call | solution.py:320
  466.4 7.1 %place.3 = f32[128,16,1024]{2,1,0:T(8,128)} custom-call(f32[2,128,1024]{2,1,0:T(8,128)} %get-tuple-element.145.refs_5_.refs_0_, f32[2,128,1024]{2,1,0:T(8,128)} %get-tuple-element.154.refs_6_.refs_1_, f32[2,128,1024]{2,1,0:T(8,128)} %get-tuple-element.160.refs_9_.refs_2_, ...), custom_call_target="tpu_custom_call", output_to_operand_aliasing={{}: (4, {})} | custom-call | tf_op jit(solution)/shard_map/place/pallas_call | solution.py:373
  (242 shorter events, 155.6 us)
Async XLA Ops:
  3.8 100.6 %collective-permute-start.3 = (bf16[2,512,256]{2,1,0:T(8,128)(2,1)}, bf16[2,512,256]{2,1,0:T(8,128)(2,1)}, u32[]{:S(2)}, u32[]{:S(2)}) collective-permute-start(bf16[2,512,256]{2,1,0:T(8,128)(2,1)} %get-tuple-element.95), channel_id=1, source_target_pairs={{0,16},{2,10},{4,20},{6,14},{8,24},{10,2},{12,28},{14,6},{16,0},{1... | collective-permute-start | bytes 1572872 | tf_op jit(solution)/shard_map/ppermute | solution.py:42
  11.1 93.4 %collective-permute-start.4 = (bf16[2,512,256]{2,1,0:T(8,128)(2,1)}, bf16[2,512,256]{2,1,0:T(8,128)(2,1)}, u32[]{:S(2)}, u32[]{:S(2)}) collective-permute-start(bf16[2,512,256]{2,1,0:T(8,128)(2,1)} %get-tuple-element.96), channel_id=1, source_target_pairs={{0,24},{2,18},{4,28},{6,22},{8,16},{10,26},{12,20},{14,30},{16,8},... | collective-permute-start | bytes 1572872 | tf_op jit(solution)/shard_map/ppermute | solution.py:42
  12.4 73.6 %collective-permute-start.6 = (bf16[2,512,256]{2,1,0:T(8,128)(2,1)}, bf16[2,512,256]{2,1,0:T(8,128)(2,1)}, u32[]{:S(2)}, u32[]{:S(2)}) collective-permute-start(bf16[2,512,256]{2,1,0:T(8,128)(2,1)} %get-tuple-element.86), channel_id=1, source_target_pairs={{0,16},{2,10},{4,20},{6,14},{8,24},{10,2},{12,28},{14,6},{16,0},{1... | collective-permute-start | bytes 1572872 | tf_op jit(solution)/shard_map/ppermute | solution.py:42
  14.1 82.9 %collective-permute-start.7 = (bf16[2,512,256]{2,1,0:T(8,128)(2,1)}, bf16[2,512,256]{2,1,0:T(8,128)(2,1)}, u32[]{:S(2)}, u32[]{:S(2)}) collective-permute-start(bf16[2,512,256]{2,1,0:T(8,128)(2,1)} %get-tuple-element.87), channel_id=1, source_target_pairs={{0,24},{2,18},{4,28},{6,22},{8,16},{10,26},{12,20},{14,30},{16,8},... | collective-permute-start | bytes 1572872 | tf_op jit(solution)/shard_map/ppermute | solution.py:42
  18.2 78.7 %collective-permute-start.8 = (bf16[2,512,256]{2,1,0:T(8,128)(2,1)}, bf16[2,512,256]{2,1,0:T(8,128)(2,1)}, u32[]{:S(2)}, u32[]{:S(2)}) collective-permute-start(bf16[2,512,256]{2,1,0:T(8,128)(2,1)} %get-tuple-element.88), channel_id=1, source_target_pairs={{0,8},{2,26},{4,12},{6,30},{8,0},{10,18},{12,4},{14,22},{16,24},{1... | collective-permute-start | bytes 1572872 | tf_op jit(solution)/shard_map/ppermute | solution.py:42
  110.4 63.2 %collective-permute-start.9 = (bf16[2,1024,256]{2,1,0:T(8,128)(2,1)}, bf16[2,1024,256]{2,1,0:T(8,128)(2,1)}, u32[]{:S(2)}, u32[]{:S(2)}) collective-permute-start(bf16[2,1024,256]{2,1,0:T(8,128)(2,1)} %beam_partial.9.refs_6_), channel_id=1, source_target_pairs={{0,1},{1,0},{2,3},{3,2},{4,5},{5,4},{6,7},{7,6},{8,9},{9,8},{10,11... | collective-permute-start | bytes 3145736 | tf_op jit(solution)/shard_map/ppermute | solution.py:24
  111.0 40.1 %collective-permute-start.10 = (bf16[2,512,256]{2,1,0:T(8,128)(2,1)}, bf16[2,512,256]{2,1,0:T(8,128)(2,1)}, u32[]{:S(2)}, u32[]{:S(2)}) collective-permute-start(bf16[2,512,256]{2,1,0:T(8,128)(2,1)} %get-tuple-element.101), channel_id=1, source_target_pairs={{0,16},{2,10},{4,20},{6,14},{8,24},{10,2},{12,28},{14,6},{16,0},{1... | collective-permute-start | bytes 1572872 | tf_op jit(solution)/shard_map/ppermute | solution.py:42
  115.5 38.9 %collective-permute-start.11 = (bf16[2,512,256]{2,1,0:T(8,128)(2,1)}, bf16[2,512,256]{2,1,0:T(8,128)(2,1)}, u32[]{:S(2)}, u32[]{:S(2)}) collective-permute-start(bf16[2,512,256]{2,1,0:T(8,128)(2,1)} %get-tuple-element.102), channel_id=1, source_target_pairs={{0,24},{2,18},{4,28},{6,22},{8,16},{10,26},{12,20},{14,30},{16,8},... | collective-permute-start | bytes 1572872 | tf_op jit(solution)/shard_map/ppermute | solution.py:42
  116.0 57.2 %collective-permute-start.12 = (bf16[2,512,256]{2,1,0:T(8,128)(2,1)}, bf16[2,512,256]{2,1,0:T(8,128)(2,1)}, u32[]{:S(2)}, u32[]{:S(2)}) collective-permute-start(bf16[2,512,256]{2,1,0:T(8,128)(2,1)} %get-tuple-element.103), channel_id=1, source_target_pairs={{0,8},{2,26},{4,12},{6,30},{8,0},{10,18},{12,4},{14,22},{16,24},{1... | collective-permute-start | bytes 1572872 | tf_op jit(solution)/shard_map/ppermute | solution.py:42
  128.6 45.2 %collective-permute-start.17 = (bf16[2,2,128,256]{3,2,1,0:T(8,128)(2,1)}, bf16[2,2,128,256]{3,2,1,0:T(8,128)(2,1)S(1)}, u32[]{:S(2)}, u32[]{:S(2)}) collective-permute-start(bf16[2,2,128,256]{3,2,1,0:T(8,128)(2,1)} %get-tuple-element.109), channel_id=1, source_target_pairs={{0,2},{2,4},{4,6},{6,0},{1,3},{3,5},{5,7},{7,1},{8,10},{10,12},{12... | collective-permute-start | bytes 786440 | tf_op jit(solution)/shard_map/ppermute | solution.py:24
  151.1 28.8 %collective-permute-start.18 = (bf16[2,2,128,256]{3,2,1,0:T(8,128)(2,1)}, bf16[2,2,128,256]{3,2,1,0:T(8,128)(2,1)}, u32[]{:S(2)}, u32[]{:S(2)}) collective-permute-start(bf16[2,2,128,256]{3,2,1,0:T(8,128)(2,1)} %get-tuple-element.110), channel_id=1, source_target_pairs={{0,4},{2,6},{4,0},{6,2},{1,5},{3,7},{5,1},{7,3},{8,12},{10,14},{12... | collective-permute-start | bytes 786440 | tf_op jit(solution)/shard_map/ppermute | solution.py:24
  154.4 46.9 %collective-permute-start.21 = (bf16[2,512,256]{2,1,0:T(8,128)(2,1)S(1)}, bf16[2,512,256]{2,1,0:T(8,128)(2,1)S(1)}, u32[]{:S(2)}, u32[]{:S(2)}) collective-permute-start(bf16[2,512,256]{2,1,0:T(8,128)(2,1)S(1)} %copy-done.20), channel_id=1, source_target_pairs={{0,16},{2,10},{4,20},{6,14},{8,24},{10,2},{12,28},{14,6},{16,0},{1... | collective-permute-start | bytes 1572872 | tf_op jit(solution)/shard_map/ppermute | solution.py:42
  173.1 28.2 %collective-permute-start.22 = (bf16[2,512,256]{2,1,0:T(8,128)(2,1)S(1)}, bf16[2,512,256]{2,1,0:T(8,128)(2,1)S(1)}, u32[]{:S(2)}, u32[]{:S(2)}) collective-permute-start(bf16[2,512,256]{2,1,0:T(8,128)(2,1)S(1)} %copy-done.21), channel_id=1, source_target_pairs={{0,24},{2,18},{4,28},{6,22},{8,16},{10,26},{12,20},{14,30},{16,8},... | collective-permute-start | bytes 1572872 | tf_op jit(solution)/shard_map/ppermute | solution.py:42
  173.6 27.8 %collective-permute-start.23 = (bf16[2,512,256]{2,1,0:T(8,128)(2,1)}, bf16[2,512,256]{2,1,0:T(8,128)(2,1)S(1)}, u32[]{:S(2)}, u32[]{:S(2)}) collective-permute-start(bf16[2,512,256]{2,1,0:T(8,128)(2,1)} %get-tuple-element.116), channel_id=1, source_target_pairs={{0,8},{2,26},{4,12},{6,30},{8,0},{10,18},{12,4},{14,22},{16,24},{1... | collective-permute-start | bytes 1572872 | tf_op jit(solution)/shard_map/ppermute | solution.py:42
  179.8 39.5 %collective-permute-start.20 = (bf16[2,1024,256]{2,1,0:T(8,128)(2,1)}, bf16[2,1024,256]{2,1,0:T(8,128)(2,1)}, u32[]{:S(2)}, u32[]{:S(2)}) collective-permute-start(bf16[2,1024,256]{2,1,0:T(8,128)(2,1)} %beam_partial.10.refs_6_), channel_id=1, source_target_pairs={{0,1},{1,0},{2,3},{3,2},{4,5},{5,4},{6,7},{7,6},{8,9},{9,8},{10,11... | collective-permute-start | bytes 3145736 | tf_op jit(solution)/shard_map/ppermute | solution.py:24
  208.5 46.0 %collective-permute-start.31 = (bf16[2,1024,256]{2,1,0:T(8,128)(2,1)}, bf16[2,1024,256]{2,1,0:T(8,128)(2,1)}, u32[]{:S(2)}, u32[]{:S(2)}) collective-permute-start(bf16[2,1024,256]{2,1,0:T(8,128)(2,1)} %beam_partial.11.refs_6_), channel_id=1, source_target_pairs={{0,1},{1,0},{2,3},{3,2},{4,5},{5,4},{6,7},{7,6},{8,9},{9,8},{10,11... | collective-permute-start | bytes 3145736 | tf_op jit(solution)/shard_map/ppermute | solution.py:24
  219.3 32.9 %collective-permute-start.2 = (bf16[2,512,256]{2,1,0:T(8,128)(2,1)S(1)}, bf16[2,512,256]{2,1,0:T(8,128)(2,1)S(1)}, u32[]{:S(2)}, u32[]{:S(2)}) collective-permute-start(bf16[2,512,256]{2,1,0:T(8,128)(2,1)S(1)} %copy-done.22), channel_id=1, source_target_pairs={{0,8},{2,26},{4,12},{6,30},{8,0},{10,18},{12,4},{14,22},{16,24},{1... | collective-permute-start | bytes 1572872 | tf_op jit(solution)/shard_map/ppermute | solution.py:42
  234.7 46.5 %collective-permute-start.29 = (bf16[2,2,128,256]{3,2,1,0:T(8,128)(2,1)}, bf16[2,2,128,256]{3,2,1,0:T(8,128)(2,1)S(1)}, u32[]{:S(2)}, u32[]{:S(2)}) collective-permute-start(bf16[2,2,128,256]{3,2,1,0:T(8,128)(2,1)} %get-tuple-element.125), channel_id=1, source_target_pairs={{0,4},{2,6},{4,0},{6,2},{1,5},{3,7},{5,1},{7,3},{8,12},{10,14},{12... | collective-permute-start | bytes 786440 | tf_op jit(solution)/shard_map/ppermute | solution.py:24
  245.6 51.9 %collective-permute-start.25 = (bf16[2,512,256]{2,1,0:T(8,128)(2,1)}, bf16[2,512,256]{2,1,0:T(8,128)(2,1)S(1)}, u32[]{:S(2)}, u32[]{:S(2)}) collective-permute-start(bf16[2,512,256]{2,1,0:T(8,128)(2,1)} %get-tuple-element.121), channel_id=1, source_target_pairs={{0,16},{2,10},{4,20},{6,14},{8,24},{10,2},{12,28},{14,6},{16,0},{1... | collective-permute-start | bytes 1572872 | tf_op jit(solution)/shard_map/ppermute | solution.py:42
  252.2 45.4 %collective-permute-start.26 = (bf16[2,512,256]{2,1,0:T(8,128)(2,1)}, bf16[2,512,256]{2,1,0:T(8,128)(2,1)S(1)}, u32[]{:S(2)}, u32[]{:S(2)}) collective-permute-start(bf16[2,512,256]{2,1,0:T(8,128)(2,1)} %get-tuple-element.122), channel_id=1, source_target_pairs={{0,24},{2,18},{4,28},{6,22},{8,16},{10,26},{12,20},{14,30},{16,8},... | collective-permute-start | bytes 1572872 | tf_op jit(solution)/shard_map/ppermute | solution.py:42
  254.5 43.1 %collective-permute-start.27 = (bf16[2,512,256]{2,1,0:T(8,128)(2,1)}, bf16[2,512,256]{2,1,0:T(8,128)(2,1)S(1)}, u32[]{:S(2)}, u32[]{:S(2)}) collective-permute-start(bf16[2,512,256]{2,1,0:T(8,128)(2,1)} %get-tuple-element.123), channel_id=1, source_target_pairs={{0,8},{2,26},{4,12},{6,30},{8,0},{10,18},{12,4},{14,22},{16,24},{1... | collective-permute-start | bytes 1572872 | tf_op jit(solution)/shard_map/ppermute | solution.py:42
  254.5 33.6 %collective-permute-start.30 = (bf16[2,2,128,256]{3,2,1,0:T(8,128)(2,1)S(1)}, bf16[2,2,128,256]{3,2,1,0:T(8,128)(2,1)}, u32[]{:S(2)}, u32[]{:S(2)}) collective-permute-start(bf16[2,2,128,256]{3,2,1,0:T(8,128)(2,1)S(1)} %copy-done.28), channel_id=1, source_target_pairs={{0,6},{2,0},{4,2},{6,4},{1,7},{3,1},{5,3},{7,5},{8,14},{10,8},{12,... | collective-permute-start | bytes 786440 | tf_op jit(solution)/shard_map/ppermute | solution.py:24
  281.3 36.5 %collective-permute-start.24 = (bf16[2,1024,256]{2,1,0:T(8,128)(2,1)}, bf16[2,1024,256]{2,1,0:T(8,128)(2,1)}, u32[]{:S(2)}, u32[]{:S(2)}) collective-permute-start(bf16[2,1024,256]{2,1,0:T(8,128)(2,1)} %beam_partial.12.refs_6_), channel_id=1, source_target_pairs={{0,1},{1,0},{2,3},{3,2},{4,5},{5,4},{6,7},{7,6},{8,9},{9,8},{10,11... | collective-permute-start | bytes 3145736 | tf_op jit(solution)/shard_map/ppermute | solution.py:24
  304.7 49.4 %collective-permute-start.38 = (bf16[2,1024,256]{2,1,0:T(8,128)(2,1)}, bf16[2,1024,256]{2,1,0:T(8,128)(2,1)S(1)}, u32[]{:S(2)}, u32[]{:S(2)}) collective-permute-start(bf16[2,1024,256]{2,1,0:T(8,128)(2,1)} %beam_partial.13.refs_6_), channel_id=1, source_target_pairs={{0,1},{1,0},{2,3},{3,2},{4,5},{5,4},{6,7},{7,6},{8,9},{9,8},{10,11... | collective-permute-start | bytes 3145736 | tf_op jit(solution)/shard_map/ppermute | solution.py:24
  314.2 37.4 %collective-permute-start.40 = (bf16[2,512,256]{2,1,0:T(8,128)(2,1)}, bf16[2,512,256]{2,1,0:T(8,128)(2,1)S(1)}, u32[]{:S(2)}, u32[]{:S(2)}) collective-permute-start(bf16[2,512,256]{2,1,0:T(8,128)(2,1)} %get-tuple-element.141), channel_id=1, source_target_pairs={{0,24},{2,18},{4,28},{6,22},{8,16},{10,26},{12,20},{14,30},{16,8},... | collective-permute-start | bytes 1572872 | tf_op jit(solution)/shard_map/ppermute | solution.py:42
  317.8 33.9 %collective-permute-start.41 = (bf16[2,512,256]{2,1,0:T(8,128)(2,1)}, bf16[2,512,256]{2,1,0:T(8,128)(2,1)S(1)}, u32[]{:S(2)}, u32[]{:S(2)}) collective-permute-start(bf16[2,512,256]{2,1,0:T(8,128)(2,1)} %get-tuple-element.142), channel_id=1, source_target_pairs={{0,8},{2,26},{4,12},{6,30},{8,0},{10,18},{12,4},{14,22},{16,24},{1... | collective-permute-start | bytes 1572872 | tf_op jit(solution)/shard_map/ppermute | solution.py:42
  334.7 29.1 %collective-permute-start.33 = (bf16[2,2,128,256]{3,2,1,0:T(8,128)(2,1)}, bf16[2,2,128,256]{3,2,1,0:T(8,128)(2,1)}, u32[]{:S(2)}, u32[]{:S(2)}) collective-permute-start(bf16[2,2,128,256]{3,2,1,0:T(8,128)(2,1)} %get-tuple-element.132), channel_id=1, source_target_pairs={{0,4},{2,6},{4,0},{6,2},{1,5},{3,7},{5,1},{7,3},{8,12},{10,14},{12... | collective-permute-start | bytes 786440 | tf_op jit(solution)/shard_map/ppermute | solution.py:24
  351.6 38.6 %collective-permute-start.48 = (bf16[2,512,256]{2,1,0:T(8,128)(2,1)}, bf16[2,512,256]{2,1,0:T(8,128)(2,1)S(1)}, u32[]{:S(2)}, u32[]{:S(2)}) collective-permute-start(bf16[2,512,256]{2,1,0:T(8,128)(2,1)} %get-tuple-element.99.refs_5_), channel_id=1, source_target_pairs={{0,8},{2,26},{4,12},{6,30},{8,0},{10,18},{12,4},{14,22},{16,24},{1... | collective-permute-start | bytes 1572872 | tf_op jit(solution)/shard_map/ppermute | solution.py:42
  351.7 38.4 %collective-permute-start.46 = (bf16[2,512,256]{2,1,0:T(8,128)(2,1)}, bf16[2,512,256]{2,1,0:T(8,128)(2,1)S(1)}, u32[]{:S(2)}, u32[]{:S(2)}) collective-permute-start(bf16[2,512,256]{2,1,0:T(8,128)(2,1)} %get-tuple-element.151), channel_id=1, source_target_pairs={{0,16},{2,10},{4,20},{6,14},{8,24},{10,2},{12,28},{14,6},{16,0},{1... | collective-permute-start | bytes 1572872 | tf_op jit(solution)/shard_map/ppermute | solution.py:42
  355.1 35.0 %collective-permute-start.47 = (bf16[2,512,256]{2,1,0:T(8,128)(2,1)}, bf16[2,512,256]{2,1,0:T(8,128)(2,1)S(1)}, u32[]{:S(2)}, u32[]{:S(2)}) collective-permute-start(bf16[2,512,256]{2,1,0:T(8,128)(2,1)} %get-tuple-element.152), channel_id=1, source_target_pairs={{0,24},{2,18},{4,28},{6,22},{8,16},{10,26},{12,20},{14,30},{16,8},... | collective-permute-start | bytes 1572872 | tf_op jit(solution)/shard_map/ppermute | solution.py:42
  363.8 44.2 %collective-permute-start.45 = (bf16[2,1024,256]{2,1,0:T(8,128)(2,1)}, bf16[2,1024,256]{2,1,0:T(8,128)(2,1)}, u32[]{:S(2)}, u32[]{:S(2)}) collective-permute-start(bf16[2,1024,256]{2,1,0:T(8,128)(2,1)} %beam_partial.14.refs_6_), channel_id=1, source_target_pairs={{0,1},{1,0},{2,3},{3,2},{4,5},{5,4},{6,7},{7,6},{8,9},{9,8},{10,11... | collective-permute-start | bytes 3145736 | tf_op jit(solution)/shard_map/ppermute | solution.py:24
  397.3 32.5 %collective-permute-start.52 = (bf16[2,1024,256]{2,1,0:T(8,128)(2,1)}, bf16[2,1024,256]{2,1,0:T(8,128)(2,1)S(1)}, u32[]{:S(2)}, u32[]{:S(2)}) collective-permute-start(bf16[2,1024,256]{2,1,0:T(8,128)(2,1)} %beam_partial.15.refs_6_), channel_id=1, source_target_pairs={{0,1},{1,0},{2,3},{3,2},{4,5},{5,4},{6,7},{7,6},{8,9},{9,8},{10,11... | collective-permute-start | bytes 3145736 | tf_op jit(solution)/shard_map/ppermute | solution.py:24
  (77 other events, 864.5 us)
